TPU v7x, 256 devices: a whole 4x4x8 slice. The times are simulated.
256 devices in a mesh: blk: 32 (over x, z), src: 2 (over y_lo), layer: 4 (over y_hi, core).
Axes of the slice: x: 4, y: 4 (y_hi: 2, y_lo: 2; y = y_hi * 2 + y_lo), z: 8, core: 2. Of those that a mesh axis runs over, the one named last changes fastest.
Arguments:
- resident_act: bfloat16 [4, 16384, 4096], P('layer', 'blk'), may hold values from -6 to 6
- resident_grad: bfloat16 [4, 16384, 4096], P('layer', 'blk'), may hold values from -6 to 6
- source_act: bfloat16 [4, 1024, 4096], P('layer', ('blk', 'src')), may hold values from -6 to 6
- source_grad: bfloat16 [4, 1024, 4096], P('layer', ('blk', 'src')), may hold values from -6 to 6
- probes: bfloat16 [1024, 256], P(('blk', 'src')), may hold values from -6 to 6
Outputs:
- kernel_product: float32 [16384, 256], P(('blk', 'layer'))
All inputs are finite; a program needn't handle non-finite values.
Results may differ from a plain program's by a relative error of at most 0.0029.
Values may be sent and summed in bfloat16 or wider, within the bound.
No kernel may reach another device: no remote copies, remote signals or barrier semaphores. Data moves between devices by JAX's collectives and lax.ppermute only.
A program may use at most 64 MiB of HBM per device.

v0:
```python
import jax
import jax.numpy as jnp
from jax import lax
from jax.sharding import PartitionSpec as P

LAYERS = 4


def shifted(shard, axis, by):
    length = lax.axis_size(axis)
    return lax.ppermute(shard, axis, [(i, (i + by) % length) for i in range(length)])


def contract_rows(left, right):
    return lax.dot_general(
        left, right, (((1,), (1,)), ((), ())), preferred_element_type=jnp.float32
    )


def on_device(resident_act, resident_grad, source_act, source_grad, probes):
    width = resident_act.shape[2]
    blocks = lax.axis_size("blk")
    source_total = source_act.shape[1] * blocks * lax.axis_size("src")
    inverse_width = jnp.float32(1.0 / width)

    def accumulate(total, acts, grads, probe_rows):
        act_gram = contract_rows(acts[0], resident_act[0])
        grad_gram = contract_rows(grads[0], resident_grad[0])
        kernel = (act_gram * grad_gram * inverse_width).astype(jnp.bfloat16)
        total = total + lax.dot_general(
            kernel, probe_rows, (((0,), (0,)), ((), ())), preferred_element_type=jnp.float32
        )
        return total

    total = jnp.zeros((resident_act.shape[1], probes.shape[1]), jnp.float32)

    def turn(step, carry):
        acc, acts, grads, probe_rows = carry
        acc = accumulate(acc, acts, grads, probe_rows)
        acts, grads, probe_rows = shifted((acts, grads, probe_rows), "blk", 1)
        return (acc, acts, grads, probe_rows)

    total, acts, grads, probe_rows = lax.fori_loop(
        0, blocks - 1, turn, (total, source_act, source_grad, probes)
    )
    total = accumulate(total, acts, grads, probe_rows)
    summed = lax.psum(total, "src")
    result = lax.psum_scatter(summed, "layer", scatter_dimension=0, tiled=True)
    return result * jnp.float32((LAYERS * source_total) ** (-0.5))


def solution(mesh):
    in_specs = (
        P("layer", "blk", None),
        P("layer", "blk", None),
        P("layer", ("blk", "src"), None),
        P("layer", ("blk", "src"), None),
        P(("blk", "src"), None),
    )
    out_specs = P(("blk", "layer"), None)
    return jax.shard_map(
        on_device, mesh=mesh, in_specs=in_specs, out_specs=out_specs, check_vma=False
    )
```

profile of v0, /device:TPU:1, one launch (start us, length us, event | category | flops | bytes accessed | tf_op | source)
XLA Modules:
  0.0 447.1 jit_solution(16705975416642677490)
XLA Ops:
  9.0 325.9 %while.17 = (s32[]{:T(128)}, f32[512,256]{1,0:T(8,128)S(1)}, bf16[1,16,4096]{2,1,0:T(8,128)(2,1)S(1)}, bf16[1,16,4096]{2,1,0:T(8,128)(2,1)S(1)}, bf16[16,256]{1,...) while((s32[]{:T(128)}, f32[512,256]{1,0:T(8,128)S(1)}, ...), condition=%wide.region_1.0_spmd.clone, body=%wide.region_0.0_spmd.clone.sunk | while | flops 138698752 | bytes 11395295 | solution.py:43
  18.3 3.8 convolution_add_fusion.3
  30.1 3.8 convolution_add_fusion.3
  38.4 3.8 convolution_add_fusion.3
  51.6 3.8 convolution_add_fusion.3
  61.3 3.8 convolution_add_fusion.3
  70.0 3.8 convolution_add_fusion.3
  82.7 3.8 convolution_add_fusion.3
  91.7 3.8 convolution_add_fusion.3
  101.8 3.8 convolution_add_fusion.3
  113.6 3.8 convolution_add_fusion.3
  121.9 3.8 convolution_add_fusion.3
  134.1 3.8 convolution_add_fusion.3
  144.0 3.8 convolution_add_fusion.3
  154.5 3.8 convolution_add_fusion.3
  165.2 3.8 convolution_add_fusion.3
  175.3 3.8 convolution_add_fusion.3
  184.7 3.8 convolution_add_fusion.3
  196.4 3.8 convolution_add_fusion.3
  206.6 3.8 convolution_add_fusion.3
  217.5 3.8 convolution_add_fusion.3
  227.8 3.8 convolution_add_fusion.3
  238.0 3.8 convolution_add_fusion.3
  249.5 3.8 convolution_add_fusion.3
  259.9 3.8 convolution_add_fusion.3
  269.6 3.8 convolution_add_fusion.3
  279.4 3.8 convolution_add_fusion.3
  290.0 3.8 convolution_add_fusion.3
  300.3 3.8 convolution_add_fusion.3
  338.4 4.5 %convolution_add_fusion.1 = f32[512,256]{1,0:T(8,128)} fusion(f32[512,256]{1,0:T(8,128)S(1)} %get-tuple-element.45, bf16[16,256]{1,0:T(8,128)(2,1)S(1)} %get-tuple-element.48, f32[16,512]{1,0:T(8,128)S(1)} %fusion.20, bf16[1,512,4096]{2,1,0:T(8,128)(2,1)} %get-tuple-element.160, bf16[1,16,4096]{2,1,0:T(8,128)(2,1)S(1)} %get-tuple-element.46), kind=kOutput, calls=%fused_computation.16 | convolution fusion | flops 71458816 | bytes 5414912 | tf_op jit(solution)/shard_map/dot_general | solution.py:30
  343.0 60.8 %reduce-scatter.2.cloned.1.call-done = f32[128,256]{1,0:T(8,128)} async-done(((f32[512,256]{1,0:T(8,128)}), f32[128,256]{1,0:T(8,128)}) %reduce-scatter.2.cloned.1.call-update) | async-done | bytes 131088 | tf_op jit(solution)/shard_map/reduce_scatter | solution.py:48
  403.8 34.9 %all-reduce.2.cloned.1.call-done = f32[128,256]{1,0:T(8,128)} async-done(((f32[128,256]{1,0:T(8,128)}), f32[128,256]{1,0:T(8,128)}) %all-reduce.2.cloned.1.call-update) | async-done | bytes 131088 | tf_op jit(solution)/shard_map/psum | solution.py:47
  (323 shorter events, 226.1 us)
Async XLA Ops:
  6.5 397.2 %reduce-scatter.2.cloned.1.call-start = ((), (), s32[]{:S(2)}) async-start(), calls=%async_computation.1 | async-start | bytes 655360 | tf_op jit(solution)/shard_map/reduce_scatter | solution.py:48
  9.0 13.1 %collective-permute-start.2 = (bf16[16,256]{1,0:T(8,128)(2,1)S(1)}, bf16[16,256]{1,0:T(8,128)(2,1)S(1)}, u32[]{:S(2)}, u32[]{:S(2)}) collective-permute-start(bf16[16,256]{1,0:T(8,128)(2,1)S(1)} %copy.15), channel_id=1, source_target_pairs={{0,8},{8,16},{16,24},{24,32},{32,40},{40,48},{48,56},{56,64},{64,7... | collective-permute-start | bytes 24584 | tf_op jit(solution)/shard_map/while/body/eval_jaxpr/ppermute | solution.py:11
  11.5 10.6 %collective-permute-start = (bf16[1,16,4096]{2,1,0:T(8,128)(2,1)S(1)}, bf16[1,16,4096]{2,1,0:T(8,128)(2,1)S(1)}, u32[]{:S(2)}, u32[]{:S(2)}) collective-permute-start(bf16[1,16,4096]{2,1,0:T(8,128)(2,1)S(1)} %copy.13), channel_id=1, source_target_pairs={{0,8},{8,16},{16,24},{24,32},{32,40},{40,48},{48,56},{56,64},{64,7... | collective-permute-start | bytes 393224 | tf_op jit(solution)/shard_map/while/body/eval_jaxpr/ppermute | solution.py:11
  13.2 10.6 %collective-permute-start.1 = (bf16[1,16,4096]{2,1,0:T(8,128)(2,1)S(1)}, bf16[1,16,4096]{2,1,0:T(8,128)(2,1)S(1)}, u32[]{:S(2)}, u32[]{:S(2)}) collective-permute-start(bf16[1,16,4096]{2,1,0:T(8,128)(2,1)S(1)} %copy.14), channel_id=1, source_target_pairs={{0,8},{8,16},{16,24},{24,32},{32,40},{40,48},{48,56},{56,64},{64,7... | collective-permute-start | bytes 393224 | tf_op jit(solution)/shard_map/while/body/eval_jaxpr/ppermute | solution.py:11
  23.8 10.1 %collective-permute-start.2 = (bf16[16,256]{1,0:T(8,128)(2,1)S(1)}, bf16[16,256]{1,0:T(8,128)(2,1)S(1)}, u32[]{:S(2)}, u32[]{:S(2)}) collective-permute-start(bf16[16,256]{1,0:T(8,128)(2,1)S(1)} %copy.15), channel_id=1, source_target_pairs={{0,8},{8,16},{16,24},{24,32},{32,40},{40,48},{48,56},{56,64},{64,7... | collective-permute-start | bytes 24584 | tf_op jit(solution)/shard_map/while/body/eval_jaxpr/ppermute | solution.py:11
  43.4 12.0 %collective-permute-start.2 = (bf16[16,256]{1,0:T(8,128)(2,1)S(1)}, bf16[16,256]{1,0:T(8,128)(2,1)S(1)}, u32[]{:S(2)}, u32[]{:S(2)}) collective-permute-start(bf16[16,256]{1,0:T(8,128)(2,1)S(1)} %copy.15), channel_id=1, source_target_pairs={{0,8},{8,16},{16,24},{24,32},{32,40},{40,48},{48,56},{56,64},{64,7... | collective-permute-start | bytes 24584 | tf_op jit(solution)/shard_map/while/body/eval_jaxpr/ppermute | solution.py:11
  43.6 11.8 %collective-permute-start = (bf16[1,16,4096]{2,1,0:T(8,128)(2,1)S(1)}, bf16[1,16,4096]{2,1,0:T(8,128)(2,1)S(1)}, u32[]{:S(2)}, u32[]{:S(2)}) collective-permute-start(bf16[1,16,4096]{2,1,0:T(8,128)(2,1)S(1)} %copy.13), channel_id=1, source_target_pairs={{0,8},{8,16},{16,24},{24,32},{32,40},{40,48},{48,56},{56,64},{64,7... | collective-permute-start | bytes 393224 | tf_op jit(solution)/shard_map/while/body/eval_jaxpr/ppermute | solution.py:11
  45.3 10.1 %collective-permute-start.1 = (bf16[1,16,4096]{2,1,0:T(8,128)(2,1)S(1)}, bf16[1,16,4096]{2,1,0:T(8,128)(2,1)S(1)}, u32[]{:S(2)}, u32[]{:S(2)}) collective-permute-start(bf16[1,16,4096]{2,1,0:T(8,128)(2,1)S(1)} %copy.14), channel_id=1, source_target_pairs={{0,8},{8,16},{16,24},{24,32},{32,40},{40,48},{48,56},{56,64},{64,7... | collective-permute-start | bytes 393224 | tf_op jit(solution)/shard_map/while/body/eval_jaxpr/ppermute | solution.py:11
  55.4 9.6 %collective-permute-start.2 = (bf16[16,256]{1,0:T(8,128)(2,1)S(1)}, bf16[16,256]{1,0:T(8,128)(2,1)S(1)}, u32[]{:S(2)}, u32[]{:S(2)}) collective-permute-start(bf16[16,256]{1,0:T(8,128)(2,1)S(1)} %copy.15), channel_id=1, source_target_pairs={{0,8},{8,16},{16,24},{24,32},{32,40},{40,48},{48,56},{56,64},{64,7... | collective-permute-start | bytes 24584 | tf_op jit(solution)/shard_map/while/body/eval_jaxpr/ppermute | solution.py:11
  73.9 12.6 %collective-permute-start.2 = (bf16[16,256]{1,0:T(8,128)(2,1)S(1)}, bf16[16,256]{1,0:T(8,128)(2,1)S(1)}, u32[]{:S(2)}, u32[]{:S(2)}) collective-permute-start(bf16[16,256]{1,0:T(8,128)(2,1)S(1)} %copy.15), channel_id=1, source_target_pairs={{0,8},{8,16},{16,24},{24,32},{32,40},{40,48},{48,56},{56,64},{64,7... | collective-permute-start | bytes 24584 | tf_op jit(solution)/shard_map/while/body/eval_jaxpr/ppermute | solution.py:11
  75.6 10.9 %collective-permute-start = (bf16[1,16,4096]{2,1,0:T(8,128)(2,1)S(1)}, bf16[1,16,4096]{2,1,0:T(8,128)(2,1)S(1)}, u32[]{:S(2)}, u32[]{:S(2)}) collective-permute-start(bf16[1,16,4096]{2,1,0:T(8,128)(2,1)S(1)} %copy.13), channel_id=1, source_target_pairs={{0,8},{8,16},{16,24},{24,32},{32,40},{40,48},{48,56},{56,64},{64,7... | collective-permute-start | bytes 393224 | tf_op jit(solution)/shard_map/while/body/eval_jaxpr/ppermute | solution.py:11
  106.2 11.2 %collective-permute-start.2 = (bf16[16,256]{1,0:T(8,128)(2,1)S(1)}, bf16[16,256]{1,0:T(8,128)(2,1)S(1)}, u32[]{:S(2)}, u32[]{:S(2)}) collective-permute-start(bf16[16,256]{1,0:T(8,128)(2,1)S(1)} %copy.15), channel_id=1, source_target_pairs={{0,8},{8,16},{16,24},{24,32},{32,40},{40,48},{48,56},{56,64},{64,7... | collective-permute-start | bytes 24584 | tf_op jit(solution)/shard_map/while/body/eval_jaxpr/ppermute | solution.py:11
  118.4 10.6 %collective-permute-start.1 = (bf16[1,16,4096]{2,1,0:T(8,128)(2,1)S(1)}, bf16[1,16,4096]{2,1,0:T(8,128)(2,1)S(1)}, u32[]{:S(2)}, u32[]{:S(2)}) collective-permute-start(bf16[1,16,4096]{2,1,0:T(8,128)(2,1)S(1)} %copy.14), channel_id=1, source_target_pairs={{0,8},{8,16},{16,24},{24,32},{32,40},{40,48},{48,56},{56,64},{64,7... | collective-permute-start | bytes 393224 | tf_op jit(solution)/shard_map/while/body/eval_jaxpr/ppermute | solution.py:11
  129.4 11.0 %collective-permute-start.1 = (bf16[1,16,4096]{2,1,0:T(8,128)(2,1)S(1)}, bf16[1,16,4096]{2,1,0:T(8,128)(2,1)S(1)}, u32[]{:S(2)}, u32[]{:S(2)}) collective-permute-start(bf16[1,16,4096]{2,1,0:T(8,128)(2,1)S(1)} %copy.14), channel_id=1, source_target_pairs={{0,8},{8,16},{16,24},{24,32},{32,40},{40,48},{48,56},{56,64},{64,7... | collective-permute-start | bytes 393224 | tf_op jit(solution)/shard_map/while/body/eval_jaxpr/ppermute | solution.py:11
  140.5 10.4 %collective-permute-start.1 = (bf16[1,16,4096]{2,1,0:T(8,128)(2,1)S(1)}, bf16[1,16,4096]{2,1,0:T(8,128)(2,1)S(1)}, u32[]{:S(2)}, u32[]{:S(2)}) collective-permute-start(bf16[1,16,4096]{2,1,0:T(8,128)(2,1)S(1)} %copy.14), channel_id=1, source_target_pairs={{0,8},{8,16},{16,24},{24,32},{32,40},{40,48},{48,56},{56,64},{64,7... | collective-permute-start | bytes 393224 | tf_op jit(solution)/shard_map/while/body/eval_jaxpr/ppermute | solution.py:11
  169.2 9.9 %collective-permute-start.2 = (bf16[16,256]{1,0:T(8,128)(2,1)S(1)}, bf16[16,256]{1,0:T(8,128)(2,1)S(1)}, u32[]{:S(2)}, u32[]{:S(2)}) collective-permute-start(bf16[16,256]{1,0:T(8,128)(2,1)S(1)} %copy.15), channel_id=1, source_target_pairs={{0,8},{8,16},{16,24},{24,32},{32,40},{40,48},{48,56},{56,64},{64,7... | collective-permute-start | bytes 24584 | tf_op jit(solution)/shard_map/while/body/eval_jaxpr/ppermute | solution.py:11
  188.8 11.4 %collective-permute-start.2 = (bf16[16,256]{1,0:T(8,128)(2,1)S(1)}, bf16[16,256]{1,0:T(8,128)(2,1)S(1)}, u32[]{:S(2)}, u32[]{:S(2)}) collective-permute-start(bf16[16,256]{1,0:T(8,128)(2,1)S(1)} %copy.15), channel_id=1, source_target_pairs={{0,8},{8,16},{16,24},{24,32},{32,40},{40,48},{48,56},{56,64},{64,7... | collective-permute-start | bytes 24584 | tf_op jit(solution)/shard_map/while/body/eval_jaxpr/ppermute | solution.py:11
  200.2 10.2 %collective-permute-start.2 = (bf16[16,256]{1,0:T(8,128)(2,1)S(1)}, bf16[16,256]{1,0:T(8,128)(2,1)S(1)}, u32[]{:S(2)}, u32[]{:S(2)}) collective-permute-start(bf16[16,256]{1,0:T(8,128)(2,1)S(1)} %copy.15), channel_id=1, source_target_pairs={{0,8},{8,16},{16,24},{24,32},{32,40},{40,48},{48,56},{56,64},{64,7... | collective-permute-start | bytes 24584 | tf_op jit(solution)/shard_map/while/body/eval_jaxpr/ppermute | solution.py:11
  210.8 10.5 %collective-permute-start.2 = (bf16[16,256]{1,0:T(8,128)(2,1)S(1)}, bf16[16,256]{1,0:T(8,128)(2,1)S(1)}, u32[]{:S(2)}, u32[]{:S(2)}) collective-permute-start(bf16[16,256]{1,0:T(8,128)(2,1)S(1)} %copy.15), channel_id=1, source_target_pairs={{0,8},{8,16},{16,24},{24,32},{32,40},{40,48},{48,56},{56,64},{64,7... | collective-permute-start | bytes 24584 | tf_op jit(solution)/shard_map/while/body/eval_jaxpr/ppermute | solution.py:11
  211.5 9.9 %collective-permute-start = (bf16[1,16,4096]{2,1,0:T(8,128)(2,1)S(1)}, bf16[1,16,4096]{2,1,0:T(8,128)(2,1)S(1)}, u32[]{:S(2)}, u32[]{:S(2)}) collective-permute-start(bf16[1,16,4096]{2,1,0:T(8,128)(2,1)S(1)} %copy.13), channel_id=1, source_target_pairs={{0,8},{8,16},{16,24},{24,32},{32,40},{40,48},{48,56},{56,64},{64,7... | collective-permute-start | bytes 393224 | tf_op jit(solution)/shard_map/while/body/eval_jaxpr/ppermute | solution.py:11
  221.4 10.2 %collective-permute-start.2 = (bf16[16,256]{1,0:T(8,128)(2,1)S(1)}, bf16[16,256]{1,0:T(8,128)(2,1)S(1)}, u32[]{:S(2)}, u32[]{:S(2)}) collective-permute-start(bf16[16,256]{1,0:T(8,128)(2,1)S(1)} %copy.15), channel_id=1, source_target_pairs={{0,8},{8,16},{16,24},{24,32},{32,40},{40,48},{48,56},{56,64},{64,7... | collective-permute-start | bytes 24584 | tf_op jit(solution)/shard_map/while/body/eval_jaxpr/ppermute | solution.py:11
  231.6 10.2 %collective-permute-start.2 = (bf16[16,256]{1,0:T(8,128)(2,1)S(1)}, bf16[16,256]{1,0:T(8,128)(2,1)S(1)}, u32[]{:S(2)}, u32[]{:S(2)}) collective-permute-start(bf16[16,256]{1,0:T(8,128)(2,1)S(1)} %copy.15), channel_id=1, source_target_pairs={{0,8},{8,16},{16,24},{24,32},{32,40},{40,48},{48,56},{56,64},{64,7... | collective-permute-start | bytes 24584 | tf_op jit(solution)/shard_map/while/body/eval_jaxpr/ppermute | solution.py:11
  241.9 11.5 %collective-permute-start.2 = (bf16[16,256]{1,0:T(8,128)(2,1)S(1)}, bf16[16,256]{1,0:T(8,128)(2,1)S(1)}, u32[]{:S(2)}, u32[]{:S(2)}) collective-permute-start(bf16[16,256]{1,0:T(8,128)(2,1)S(1)} %copy.15), channel_id=1, source_target_pairs={{0,8},{8,16},{16,24},{24,32},{32,40},{40,48},{48,56},{56,64},{64,7... | collective-permute-start | bytes 24584 | tf_op jit(solution)/shard_map/while/body/eval_jaxpr/ppermute | solution.py:11
  242.5 10.9 %collective-permute-start = (bf16[1,16,4096]{2,1,0:T(8,128)(2,1)S(1)}, bf16[1,16,4096]{2,1,0:T(8,128)(2,1)S(1)}, u32[]{:S(2)}, u32[]{:S(2)}) collective-permute-start(bf16[1,16,4096]{2,1,0:T(8,128)(2,1)S(1)} %copy.13), channel_id=1, source_target_pairs={{0,8},{8,16},{16,24},{24,32},{32,40},{40,48},{48,56},{56,64},{64,7... | collective-permute-start | bytes 393224 | tf_op jit(solution)/shard_map/while/body/eval_jaxpr/ppermute | solution.py:11
  253.4 10.3 %collective-permute-start.2 = (bf16[16,256]{1,0:T(8,128)(2,1)S(1)}, bf16[16,256]{1,0:T(8,128)(2,1)S(1)}, u32[]{:S(2)}, u32[]{:S(2)}) collective-permute-start(bf16[16,256]{1,0:T(8,128)(2,1)S(1)} %copy.15), channel_id=1, source_target_pairs={{0,8},{8,16},{16,24},{24,32},{32,40},{40,48},{48,56},{56,64},{64,7... | collective-permute-start | bytes 24584 | tf_op jit(solution)/shard_map/while/body/eval_jaxpr/ppermute | solution.py:11
  253.5 10.2 %collective-permute-start = (bf16[1,16,4096]{2,1,0:T(8,128)(2,1)S(1)}, bf16[1,16,4096]{2,1,0:T(8,128)(2,1)S(1)}, u32[]{:S(2)}, u32[]{:S(2)}) collective-permute-start(bf16[1,16,4096]{2,1,0:T(8,128)(2,1)S(1)} %copy.13), channel_id=1, source_target_pairs={{0,8},{8,16},{16,24},{24,32},{32,40},{40,48},{48,56},{56,64},{64,7... | collective-permute-start | bytes 393224 | tf_op jit(solution)/shard_map/while/body/eval_jaxpr/ppermute | solution.py:11
  266.1 9.7 %collective-permute-start.1 = (bf16[1,16,4096]{2,1,0:T(8,128)(2,1)S(1)}, bf16[1,16,4096]{2,1,0:T(8,128)(2,1)S(1)}, u32[]{:S(2)}, u32[]{:S(2)}) collective-permute-start(bf16[1,16,4096]{2,1,0:T(8,128)(2,1)S(1)} %copy.14), channel_id=1, source_target_pairs={{0,8},{8,16},{16,24},{24,32},{32,40},{40,48},{48,56},{56,64},{64,7... | collective-permute-start | bytes 393224 | tf_op jit(solution)/shard_map/while/body/eval_jaxpr/ppermute | solution.py:11
  276.0 10.0 %collective-permute-start.1 = (bf16[1,16,4096]{2,1,0:T(8,128)(2,1)S(1)}, bf16[1,16,4096]{2,1,0:T(8,128)(2,1)S(1)}, u32[]{:S(2)}, u32[]{:S(2)}) collective-permute-start(bf16[1,16,4096]{2,1,0:T(8,128)(2,1)S(1)} %copy.14), channel_id=1, source_target_pairs={{0,8},{8,16},{16,24},{24,32},{32,40},{40,48},{48,56},{56,64},{64,7... | collective-permute-start | bytes 393224 | tf_op jit(solution)/shard_map/while/body/eval_jaxpr/ppermute | solution.py:11
  304.1 10.8 %collective-permute-start.2 = (bf16[16,256]{1,0:T(8,128)(2,1)S(1)}, bf16[16,256]{1,0:T(8,128)(2,1)S(1)}, u32[]{:S(2)}, u32[]{:S(2)}) collective-permute-start(bf16[16,256]{1,0:T(8,128)(2,1)S(1)} %copy.15), channel_id=1, source_target_pairs={{0,8},{8,16},{16,24},{24,32},{32,40},{40,48},{48,56},{56,64},{64,7... | collective-permute-start | bytes 24584 | tf_op jit(solution)/shard_map/while/body/eval_jaxpr/ppermute | solution.py:11
  305.0 10.0 %collective-permute-start = (bf16[1,16,4096]{2,1,0:T(8,128)(2,1)S(1)}, bf16[1,16,4096]{2,1,0:T(8,128)(2,1)S(1)}, u32[]{:S(2)}, u32[]{:S(2)}) collective-permute-start(bf16[1,16,4096]{2,1,0:T(8,128)(2,1)S(1)} %copy.13), channel_id=1, source_target_pairs={{0,8},{8,16},{16,24},{24,32},{32,40},{40,48},{48,56},{56,64},{64,7... | collective-permute-start | bytes 393224 | tf_op jit(solution)/shard_map/while/body/eval_jaxpr/ppermute | solution.py:11
  324.9 10.1 %collective-permute-start.2 = (bf16[16,256]{1,0:T(8,128)(2,1)S(1)}, bf16[16,256]{1,0:T(8,128)(2,1)S(1)}, u32[]{:S(2)}, u32[]{:S(2)}) collective-permute-start(bf16[16,256]{1,0:T(8,128)(2,1)S(1)} %copy.15), channel_id=1, source_target_pairs={{0,8},{8,16},{16,24},{24,32},{32,40},{40,48},{48,56},{56,64},{64,7... | collective-permute-start | bytes 24584 | tf_op jit(solution)/shard_map/while/body/eval_jaxpr/ppermute | solution.py:11
  342.9 95.8 %all-reduce.2.cloned.1.call-start = ((), (), s32[]{:S(2)}) async-start(), calls=%async_computation.2 | async-start | bytes 262144 | tf_op jit(solution)/shard_map/psum | solution.py:47
  (63 other events, 530.6 us)
Sparse Core Ops, SparseCore 0:
  343.0 60.6 reduce-scatter.1
  406.3 32.3 all-reduce.1
where the time goes:
time: 450 us; the launch traced here: 447 us
  matrix products  229 us (51%)
  waiting for transfers between devices  122 us (27%)
  starting transfers between devices  76.5 us (17%)
  between operations  13.4 us (3%)
    dot_general x32, matrix products, accumulate(): lax.dot_general(kernel, probe_rows, (((0,), (0,)), ((), ())), preferred_e...  122 us
    dot_general x32, matrix products, contract_rows(): lax.dot_general(left, right, (((1,), (1,)), ((), ())), preferred_element_...  108 us
    ppermute x93, starting transfers between devices, shifted(): lax.ppermute(shard, axis, [(i, (i + by) % length) for i in range(length)])  76.4 us
    reduce_scatter x1, waiting for transfers between devices, on_device(): result = lax.psum_scatter(summed, 'layer', scatter_dimension=0, tiled=True)  60.8 us
    psum x1, waiting for transfers between devices, on_device(): summed = lax.psum(total, 'src')  34.9 us
    ppermute x93, waiting for transfers between devices, shifted(): lax.ppermute(shard, axis, [(i, (i + by) % length) for i in range(length)])  25.8 us
  transfers between devices with their start and end apart: 95, of which 22 were waited for; matrix products, arithmetic and copies ran while one was open for 50% of the time, Pallas kernels for 0%

commit v1 on v0

v1 whole, which is shorter than its diff:
```python
import jax
import jax.numpy as jnp
from jax import lax
from jax.sharding import PartitionSpec as P

LAYERS = 4


def contract_rows(left, right):
    return lax.dot_general(
        left, right, (((1,), (1,)), ((), ())), preferred_element_type=jnp.float32
    )


def on_device(resident_act, resident_grad, source_act, source_grad, probes):
    width = resident_act.shape[2]
    blocks = lax.axis_size("blk")
    source_total = source_act.shape[1] * blocks * lax.axis_size("src")
    inverse_width = jnp.float32(1.0 / width)

    probe_rows = lax.all_gather(probes, "blk", axis=0, tiled=True)
    acts = lax.all_gather(source_act[0], "blk", axis=0, tiled=True)
    grads = lax.all_gather(source_grad[0], "blk", axis=0, tiled=True)
    act_gram = contract_rows(acts, resident_act[0])
    grad_gram = contract_rows(grads, resident_grad[0])
    kernel = (act_gram * grad_gram * inverse_width).astype(jnp.bfloat16)
    total = lax.dot_general(
        kernel, probe_rows, (((0,), (0,)), ((), ())), preferred_element_type=jnp.float32
    )
    part = lax.psum_scatter(total, "layer", scatter_dimension=0, tiled=True)
    result = lax.psum(part, "src")
    return result * jnp.float32((LAYERS * source_total) ** (-0.5))


def solution(mesh):
    in_specs = (
        P("layer", "blk", None),
        P("layer", "blk", None),
        P("layer", ("blk", "src"), None),
        P("layer", ("blk", "src"), None),
        P(("blk", "src"), None),
    )
    out_specs = P(("blk", "layer"), None)
    return jax.shard_map(
        on_device, mesh=mesh, in_specs=in_specs, out_specs=out_specs, check_vma=False
    )
```

time: 450 us -> 257 us (0.57)
  matrix products: 229 us -> 12.9 us
  starting transfers between devices: 76.5 us -> 0.12 us
  waiting for transfers between devices: 122 us -> 187 us
  blocking collectives: 0 us -> 42 us
    all_gather x0 -> x2, waiting for transfers between devices: none -> 117 us  [the longest x1 75.3 us: on_device(): acts = lax.all_gather(source_act[0], 'blk', axis=0, tiled=True)]
    dot_general x32 -> x1, matrix products: 122 us -> 7.07 us  [on_device(): lax.dot_general(kernel, probe_rows, (((0,), (0,)), ((), ())), preferred_e...]
    dot_general x32 -> x1, matrix products: 108 us -> 5.82 us  [contract_rows(): lax.dot_general(left, right, (((1,), (1,)), ((), ())), preferred_element_...]
    ppermute x93 -> x0, starting transfers between devices: 76.4 us -> none  [shifted(): lax.ppermute(shard, axis, [(i, (i + by) % length) for i in range(length)])]
    all_gather x0 -> x1, blocking collectives: none -> 42 us  [on_device(): probe_rows = lax.all_gather(probes, 'blk', axis=0, tiled=True)]
    reduce_scatter x1, waiting for transfers between devices: 60.8 us -> 34 us  [on_device(): part = lax.psum_scatter(total, 'layer', scatter_dimension=0, tiled=True)]
    ppermute x93 -> x0, waiting for transfers between devices: 25.8 us -> none  [shifted(): lax.ppermute(shard, axis, [(i, (i + by) % length) for i in range(length)])]
  transfers between devices with their start and end apart: 95 -> 4, of which waited for: 22 -> 4; matrix products, arithmetic and copies ran while one was open for 50% -> 2% of each run, Pallas kernels for 0% -> 0%
where the time goes in v1:
time: 257 us
  waiting for transfers between devices  187 us (73%)
  blocking collectives  42 us (16%)
  between operations  13.1 us (5%)
  matrix products  12.9 us (5%)
    all_gather x1, waiting for transfers between devices, on_device(): acts = lax.all_gather(source_act[0], 'blk', axis=0, tiled=True)  75.3 us
    all_gather x1, blocking collectives, on_device(): probe_rows = lax.all_gather(probes, 'blk', axis=0, tiled=True)  42 us
    all_gather x1, waiting for transfers between devices, on_device(): grads = lax.all_gather(source_grad[0], 'blk', axis=0, tiled=True)  41.9 us
    psum x1, waiting for transfers between devices, on_device(): result = lax.psum(part, 'src')  34.8 us
    reduce_scatter x1, waiting for transfers between devices, on_device(): part = lax.psum_scatter(total, 'layer', scatter_dimension=0, tiled=True)  34 us
    dot_general x1, matrix products, on_device(): lax.dot_general(kernel, probe_rows, (((0,), (0,)), ((), ())), preferred_e...  7.07 us
    dot_general x1, matrix products, contract_rows(): lax.dot_general(left, right, (((1,), (1,)), ((), ())), preferred_element_...  5.82 us
  transfers between devices with their start and end apart: 4, of which 4 were waited for; matrix products, arithmetic and copies ran while one was open for 2% of the time, Pallas kernels for 0%

profile of v1, /device:TPU:1, one launch (start us, length us, event | category | flops | bytes accessed | tf_op | source)
XLA Modules:
  0.0 257.1 jit_solution(9820898550968278613)
XLA Ops:
  6.5 0.0 all-gather.7.cloned.1.call-start
  6.5 0.7 all-gather.7.cloned.1.call-update
  7.3 0.0 all-gather.5.cloned.1.call-start
  7.3 0.7 all-gather.5.cloned.1.call-update
  8.0 0.0 reduce-scatter.2.cloned.1.call-start
  8.1 42.0 %all_gather.11 = bf16[512,256]{1,0:T(8,128)(2,1)S(1)} all-gather(bf16[16,256]{1,0:T(8,128)(2,1)} %param.9), channel_id=1, replica_groups=mesh['blk'=32,'src'=2,'layer'=4] {'blk'}, dimensions={0}, use_global_device_ids=true | all-gather | bytes 270336 | tf_op jit(solution)/shard_map/all_gather | solution.py:21
  50.0 41.9 %all-gather.7.cloned.1.call-done = bf16[1,512,4096]{2,1,0:T(8,128)(2,1)} async-done(((bf16[1,16,4096]{2,1,0:T(8,128)(2,1)}), bf16[1,512,4096]{2,1,0:T(8,128)(2,1)}) %all-gather.7.cloned.1.call-update) | async-done | bytes 4194320 | tf_op jit(solution)/shard_map/all_gather | solution.py:23
  91.9 5.8 %fusion = f32[512,512]{1,0:T(8,128)S(1)} fusion(bf16[1,512,4096]{2,1,0:T(8,128)(2,1)} %param.6, bf16[1,512,4096]{2,1,0:T(8,128)(2,1)} %all-gather.7.cloned.1.call-done), kind=kOutput, calls=%fused_computation | convolution fusion | flops 2147483648 | bytes 9437184 | tf_op jit(solution)/shard_map/dot_general | solution.py:10
  97.8 75.3 %all-gather.5.cloned.1.call-done = bf16[1,512,4096]{2,1,0:T(8,128)(2,1)} async-done(((bf16[1,16,4096]{2,1,0:T(8,128)(2,1)}), bf16[1,512,4096]{2,1,0:T(8,128)(2,1)}) %all-gather.5.cloned.1.call-update) | async-done | bytes 4194320 | tf_op jit(solution)/shard_map/all_gather | solution.py:22
  173.0 7.1 %fusion.23 = f32[512,256]{1,0:T(8,128)} fusion(bf16[512,256]{1,0:T(8,128)(2,1)S(1)} %all_gather.11, f32[512,512]{1,0:T(8,128)S(1)} %fusion, bf16[1,512,4096]{2,1,0:T(8,128)(2,1)} %param.5, bf16[1,512,4096]{2,1,0:T(8,128)(2,1)} %all-gather.5.cloned.1.call-done), kind=kOutput, calls=%fused_computation.9 | convolution fusion | flops 2282487808 | bytes 10223616 | tf_op jit(solution)/shard_map/dot_general | solution.py:27
  180.1 0.0 reduce-scatter.2.cloned.1.call-update
  180.1 0.0 all-reduce.2.cloned.1.call-start
  180.2 34.0 %reduce-scatter.2.cloned.1.call-done = f32[128,256]{1,0:T(8,128)} async-done(((f32[512,256]{1,0:T(8,128)}), f32[128,256]{1,0:T(8,128)}) %reduce-scatter.2.cloned.1.call-update) | async-done | bytes 131088 | tf_op jit(solution)/shard_map/reduce_scatter | solution.py:30
  214.2 0.0 all-reduce.2.cloned.1.call-update
  214.2 34.8 %all-reduce.2.cloned.1.call-done = f32[128,256]{1,0:T(8,128)} async-done(((f32[128,256]{1,0:T(8,128)}), f32[128,256]{1,0:T(8,128)}) %all-reduce.2.cloned.1.call-update) | async-done | bytes 131088 | tf_op jit(solution)/shard_map/psum | solution.py:31
  249.0 1.6 broadcast_multiply_fusion
Async XLA Ops:
  6.5 85.4 %all-gather.7.cloned.1.call-start = ((), (), s32[]{:S(2)}) async-start(), calls=%async_computation.4 | async-start | bytes 4325376 | tf_op jit(solution)/shard_map/all_gather | solution.py:23
  7.3 165.8 %all-gather.5.cloned.1.call-start = ((), (), s32[]{:S(2)}) async-start(), calls=%async_computation.3 | async-start | bytes 4325376 | tf_op jit(solution)/shard_map/all_gather | solution.py:22
  8.0 206.1 %reduce-scatter.2.cloned.1.call-start = ((), (), s32[]{:S(2)}) async-start(), calls=%async_computation.1 | async-start | bytes 655360 | tf_op jit(solution)/shard_map/reduce_scatter | solution.py:30
  180.1 68.9 %all-reduce.2.cloned.1.call-start = ((), (), s32[]{:S(2)}) async-start(), calls=%async_computation.2 | async-start | bytes 262144 | tf_op jit(solution)/shard_map/psum | solution.py:31
Sparse Core Ops, SparseCore 0:
  9.9 81.9 all-gather.6
  94.5 78.4 all-gather.4
  180.3 33.8 reduce-scatter.1
  216.6 32.3 all-reduce.1

commit v2 on v1

v2 whole, which is shorter than its diff:
```python
import functools

import jax
import jax.numpy as jnp
from jax import lax
from jax.experimental import pallas as pl
from jax.experimental.pallas import tpu as pltpu
from jax.sharding import PartitionSpec as P


LAYERS = 4
ACROSS, ALONG = 4, 8
HOPS = {"zp": (0, 1), "zm": (0, -1), "xp": (1, 0), "xm": (-1, 0)}
ROUTE = (
    ("zp", (0, 0)),
    ("xp", (0, 0)),
    ("xm", (0, 0)),
    ("zm", (0, 0)),
    ("zp", (0, 1)),
    ("xp", (1, 0)),
    ("xm", (0, 1)),
    ("zm", (0, 7)),
    ("zp", (1, 0)),
    ("xp", (0, 7)),
    ("xm", (0, 2)),
    ("zm", (2, 0)),
    ("zp", (2, 0)),
    ("xp", (0, 6)),
    ("xm", (0, 6)),
    ("zm", (0, 6)),
    ("zp", (3, 2)),
    ("xp", (0, 2)),
    ("xm", (3, 2)),
    ("zm", (1, 6)),
    ("zp", (0, 2)),
    ("xp", (1, 6)),
    ("xm", (3, 3)),
    ("zm", (0, 5)),
    ("zp", (3, 3)),
    ("xp", (1, 5)),
    ("xm", (0, 5)),
    ("zm", (1, 5)),
    ("zp", (2, 3)),
    ("xp", (0, 3)),
    ("xm", (0, 7)),
)
CHUNKS = (16, 8, 8)


def hop_pairs(hop):
    dx, dz = HOPS[hop]
    return [
        (x * ALONG + z, (x + dx) % ACROSS * ALONG + (z + dz) % ALONG)
        for x in range(ACROSS)
        for z in range(ALONG)
    ]


def moved(offset, hop):
    dx, dz = HOPS[hop]
    return ((offset[0] + dx) % ACROSS, (offset[1] + dz) % ALONG)


def chunk_kernel(count, width, inverse_width, first, *refs):
    res_act, res_grad = refs[:2]
    blocks = refs[2 : 2 + count]
    rest = refs[2 + count :]
    if first:
        out, rows = rest
    else:
        before, out, rows = rest
    depth = blocks[0].shape[0]
    for i, block in enumerate(blocks):
        rows[i * depth : (i + 1) * depth, :] = block[...]

    def contract(left, right):
        return lax.dot_general(
            left, right, (((1,), (1,)), ((), ())), preferred_element_type=jnp.float32
        )

    act_gram = contract(res_act[...], rows[:, :width])
    grad_gram = contract(res_grad[...], rows[:, width : 2 * width])
    kernel = (act_gram * grad_gram * inverse_width).astype(jnp.bfloat16)
    part = jnp.dot(kernel, rows[:, 2 * width :], preferred_element_type=jnp.float32)
    if first:
        out[...] = part
    else:
        out[...] = before[...] + part


def add_chunk(total, res_act, res_grad, blocks):
    width = res_act.shape[1]
    first = total is None
    operands = [res_act, res_grad, *blocks] + ([] if first else [total])
    depth, wide = blocks[0].shape
    out = jax.ShapeDtypeStruct((res_act.shape[0], wide - 2 * width), jnp.float32)
    flops = 4 * res_act.shape[0] * width * depth * len(blocks)
    return pl.pallas_call(
        functools.partial(chunk_kernel, len(blocks), width, 1.0 / width, first),
        out_shape=out,
        in_specs=[pl.BlockSpec(memory_space=pltpu.VMEM)] * len(operands),
        out_specs=pl.BlockSpec(memory_space=pltpu.VMEM),
        scratch_shapes=[pltpu.VMEM((depth * len(blocks), wide), blocks[0].dtype)],
        compiler_params=pltpu.CompilerParams(vmem_limit_bytes=16 << 20),
        cost_estimate=pl.CostEstimate(flops=flops, bytes_accessed=0, transcendentals=0),
    )(*operands)


def on_device(resident_act, resident_grad, source_act, source_grad, probes):
    blocks = lax.axis_size("blk")
    source_total = source_act.shape[1] * blocks * lax.axis_size("src")
    res_act, res_grad = resident_act[0], resident_grad[0]

    own = jnp.concatenate([source_act[0], source_grad[0], probes], axis=1)
    held = {(0, 0): own}
    order = [(0, 0)]
    for hop, offset in ROUTE:
        there = moved(offset, hop)
        held[there] = lax.ppermute(held[offset], "blk", hop_pairs(hop))
        order.append(there)
    total = None
    begin = 0
    for size in CHUNKS:
        total = add_chunk(total, res_act, res_grad, [held[o] for o in order[begin : begin + size]])
        begin += size

    layer = lax.axis_index("layer")
    core, high = layer % 2, layer // 2
    pieces = total.reshape(2, 2, -1, total.shape[1])
    keep = lax.dynamic_index_in_dim(pieces, core, 1, keepdims=False)
    give = lax.dynamic_index_in_dim(pieces, 1 - core, 1, keepdims=False)
    chip = keep + lax.ppermute(give, "layer", [(l, l ^ 1) for l in range(LAYERS)])
    mine = lax.dynamic_index_in_dim(chip, high, 0, keepdims=False)
    other = lax.dynamic_index_in_dim(chip, 1 - high, 0, keepdims=False)

    def exchange(value, flip_src, flip_high):
        pairs = [
            (s * LAYERS + l, (s ^ flip_src) * LAYERS + (l ^ (2 * flip_high)))
            for s in range(2)
            for l in range(LAYERS)
        ]
        return lax.ppermute(value, ("src", "layer"), pairs)

    far = exchange(other, 0, 1)
    near = exchange(mine, 1, 0)
    wrap = exchange(other, 1, 1)
    result = mine + near + wrap + far
    return result * jnp.float32((LAYERS * source_total) ** (-0.5))


def solution(mesh):
    in_specs = (
        P("layer", "blk", None),
        P("layer", "blk", None),
        P("layer", ("blk", "src"), None),
        P("layer", ("blk", "src"), None),
        P(("blk", "src"), None),
    )
    out_specs = P(("blk", "layer"), None)
    return jax.shard_map(
        on_device, mesh=mesh, in_specs=in_specs, out_specs=out_specs, check_vma=False
    )
```

time: 257 us -> 99.5 us (0.39)
  waiting for transfers between devices: 187 us -> 29.5 us
  starting transfers between devices: 0.12 us -> 47 us
  blocking collectives: 42 us -> 0 us
  between operations: 13.1 us -> 0.17 us
  matrix products: 12.9 us -> 0 us
  local copies, waits for them, and re-layouts: 0 us -> 10.9 us
  Pallas kernels: 0 us -> 9.94 us
    all_gather x2 -> x0, waiting for transfers between devices: 117 us -> none  [the longest x1 75.3 us: on_device(): acts = lax.all_gather(source_act[0], 'blk', axis=0, tiled=True)]
    ppermute x0 -> x35, starting transfers between devices: none -> 47 us  [the longest x31 37.2 us: on_device(): held[there] = lax.ppermute(held[offset], 'blk', hop_pairs(hop))]
    all_gather x1 -> x0, blocking collectives: 42 us -> none  [on_device(): probe_rows = lax.all_gather(probes, 'blk', axis=0, tiled=True)]
    psum x1 -> x0, waiting for transfers between devices: 34.8 us -> none  [on_device(): result = lax.psum(part, 'src')]
    reduce_scatter x1 -> x0, waiting for transfers between devices: 34 us -> none  [on_device(): part = lax.psum_scatter(total, 'layer', scatter_dimension=0, tiled=True)]
    ppermute x0 -> x35, waiting for transfers between devices: none -> 29.5 us  [the longest x31 22.3 us: on_device(): held[there] = lax.ppermute(held[offset], 'blk', hop_pairs(hop))]
    dot_general x2 -> x0, matrix products: 12.9 us -> none  [the longest x1 7.07 us: on_device(): lax.dot_general(kernel, probe_rows, (((0,), (0,)), ((), ())), preferred_e...]
    unnamed x0 -> x32, local copies, waits for them, and re-layouts: none -> 10.8 us
  transfers between devices with their start and end apart: 4 -> 35, of which waited for: 4 -> 15; matrix products, arithmetic and copies ran while one was open for 2% -> 0% of each run, Pallas kernels for 0% -> 6%
where the time goes in v2:
time: 99.5 us; the launch traced here: 99.2 us
  starting transfers between devices  47 us (47%)
  waiting for transfers between devices  29.5 us (30%)
  local copies, waits for them, and re-layouts  10.9 us (11%)
  Pallas kernels  9.94 us (10%)
  other arithmetic  1.72 us (2%)
    ppermute x31, starting transfers between devices, on_device(): held[there] = lax.ppermute(held[offset], 'blk', hop_pairs(hop))  37.2 us
    ppermute x31, waiting for transfers between devices, on_device(): held[there] = lax.ppermute(held[offset], 'blk', hop_pairs(hop))  22.3 us
    unnamed x32, local copies, waits for them, and re-layouts  10.8 us
    pallas_call x3, Pallas kernels, add_chunk(): pl.pallas_call(functools.partial(chunk_kernel, len(blocks), width, 1.0 /...  9.94 us
    ppermute x3, waiting for transfers between devices, exchange(): return lax.ppermute(value, ('src', 'layer'), pairs)  6.02 us
    ppermute x1, starting transfers between devices, on_device(): lax.ppermute(give, 'layer', [(l, l ^ 1) for l in range(LAYERS)])  5.75 us
    ppermute x3, starting transfers between devices, exchange(): return lax.ppermute(value, ('src', 'layer'), pairs)  4.01 us
  transfers between devices with their start and end apart: 35, of which 15 were waited for; matrix products, arithmetic and copies ran while one was open for 0% of the time, Pallas kernels for 6%

profile of v2, /device:TPU:1, one launch (start us, length us, event | category | flops | bytes accessed | tf_op | source)
XLA Modules:
  0.0 99.2 jit_solution(342844711242954423)
XLA Ops:
  1.0 6.5 %collective-permute-start = (bf16[16,8448]{1,0:T(8,128)(2,1)S(1)}, bf16[16,8448]{1,0:T(8,128)(2,1)S(1)}, u32[]{:S(2)}, u32[]{:S(2)}) collective-permute-start(bf16[16,8448]{1,0:T(8,128)(2,1)S(1)} %pad_maximum_fusion.refs_2_), channel_id=1, source_target_pairs={{0,56},{8,0},{16,8},{24,16},{32,24},{40,32},{48,40},{56,48},{64,12... | collective-permute-start | bytes 811016 | tf_op jit(solution)/shard_map/ppermute | solution.py:119
  7.5 1.2 %collective-permute-start.22 = (bf16[16,8448]{1,0:T(8,128)(2,1)S(1)}, bf16[16,8448]{1,0:T(8,128)(2,1)S(1)}, u32[]{:S(2)}, u32[]{:S(2)}) collective-permute-start(bf16[16,8448]{1,0:T(8,128)(2,1)S(1)} %pad_maximum_fusion.refs_2_), channel_id=1, source_target_pairs={{0,64},{8,72},{16,80},{24,88},{32,96},{40,104},{48,112},{56,120},{... | collective-permute-start | bytes 811016 | tf_op jit(solution)/shard_map/ppermute | solution.py:119
  8.7 1.5 %collective-permute-start.23 = (bf16[16,8448]{1,0:T(8,128)(2,1)S(1)}, bf16[16,8448]{1,0:T(8,128)(2,1)S(1)}, u32[]{:S(2)}, u32[]{:S(2)}) collective-permute-start(bf16[16,8448]{1,0:T(8,128)(2,1)S(1)} %pad_maximum_fusion.refs_2_), channel_id=1, source_target_pairs={{0,192},{8,200},{16,208},{24,216},{32,224},{40,232},{48,240},{56,2... | collective-permute-start | bytes 811016 | tf_op jit(solution)/shard_map/ppermute | solution.py:119
  10.2 2.5 %collective-permute-done.refs_6_ = bf16[16,8448]{1,0:T(8,128)(2,1)S(1)} collective-permute-done((bf16[16,8448]{1,0:T(8,128)(2,1)S(1)}, bf16[16,8448]{1,0:T(8,128)(2,1)S(1)}, u32[]{:S(2)}, u32[]{:S(2)}) %collective-permute-start) | collective-permute-done | bytes 270368 | tf_op jit(solution)/shard_map/ppermute | solution.py:119
  12.6 3.4 %collective-permute-start.1 = (bf16[16,8448]{1,0:T(8,128)(2,1)S(1)}, bf16[16,8448]{1,0:T(8,128)(2,1)S(1)}, u32[]{:S(2)}, u32[]{:S(2)}) collective-permute-start(bf16[16,8448]{1,0:T(8,128)(2,1)S(1)} %collective-permute-done.refs_6_), channel_id=1, source_target_pairs={{0,56},{8,0},{16,8},{24,16},{32,24},{40,32},{48,40},{56,48},{64,12... | collective-permute-start | bytes 811016 | tf_op jit(solution)/shard_map/ppermute | solution.py:119
  16.1 1.3 %collective-permute-start.24 = (bf16[16,8448]{1,0:T(8,128)(2,1)S(1)}, bf16[16,8448]{1,0:T(8,128)(2,1)S(1)}, u32[]{:S(2)}, u32[]{:S(2)}) collective-permute-start(bf16[16,8448]{1,0:T(8,128)(2,1)S(1)} %collective-permute-done.22.refs_4_), channel_id=1, source_target_pairs={{0,64},{8,72},{16,80},{24,88},{32,96},{40,104},{48,112},{56,120},{... | collective-permute-start | bytes 811016 | tf_op jit(solution)/shard_map/ppermute | solution.py:119
  17.4 1.2 %collective-permute-start.27 = (bf16[16,8448]{1,0:T(8,128)(2,1)S(1)}, bf16[16,8448]{1,0:T(8,128)(2,1)S(1)}, u32[]{:S(2)}, u32[]{:S(2)}) collective-permute-start(bf16[16,8448]{1,0:T(8,128)(2,1)S(1)} %collective-permute-done.refs_6_), channel_id=1, source_target_pairs={{0,64},{8,72},{16,80},{24,88},{32,96},{40,104},{48,112},{56,120},{... | collective-permute-start | bytes 811016 | tf_op jit(solution)/shard_map/ppermute | solution.py:119
  18.6 1.5 %collective-permute-start.25 = (bf16[16,8448]{1,0:T(8,128)(2,1)S(1)}, bf16[16,8448]{1,0:T(8,128)(2,1)S(1)}, u32[]{:S(2)}, u32[]{:S(2)}) collective-permute-start(bf16[16,8448]{1,0:T(8,128)(2,1)S(1)} %collective-permute-done.4.refs_3_), channel_id=1, source_target_pairs={{0,192},{8,200},{16,208},{24,216},{32,224},{40,232},{48,240},{56,2... | collective-permute-start | bytes 811016 | tf_op jit(solution)/shard_map/ppermute | solution.py:119
  20.4 3.1 %collective-permute-done.5.refs_7_ = bf16[16,8448]{1,0:T(8,128)(2,1)S(1)} collective-permute-done((bf16[16,8448]{1,0:T(8,128)(2,1)S(1)}, bf16[16,8448]{1,0:T(8,128)(2,1)S(1)}, u32[]{:S(2)}, u32[]{:S(2)}) %collective-permute-start.5) | collective-permute-done | bytes 270368 | tf_op jit(solution)/shard_map/ppermute | solution.py:119
  23.5 2.5 %collective-permute-start.18 = (bf16[16,8448]{1,0:T(8,128)(2,1)S(1)}, bf16[16,8448]{1,0:T(8,128)(2,1)S(1)}, u32[]{:S(2)}, u32[]{:S(2)}) collective-permute-start(bf16[16,8448]{1,0:T(8,128)(2,1)S(1)} %collective-permute-done.refs_6_), channel_id=1, source_target_pairs={{0,192},{8,200},{16,208},{24,216},{32,224},{40,232},{48,240},{56,2... | collective-permute-start | bytes 811016 | tf_op jit(solution)/shard_map/ppermute | solution.py:119
  26.0 3.4 %collective-permute-done.27.refs_12_ = bf16[16,8448]{1,0:T(8,128)(2,1)S(1)} collective-permute-done((bf16[16,8448]{1,0:T(8,128)(2,1)S(1)}, bf16[16,8448]{1,0:T(8,128)(2,1)S(1)}, u32[]{:S(2)}, u32[]{:S(2)}) %collective-permute-start.27) | collective-permute-done | bytes 270368 | tf_op jit(solution)/shard_map/ppermute | solution.py:119
  29.4 1.3 %collective-permute-start.6 = (bf16[16,8448]{1,0:T(8,128)(2,1)S(1)}, bf16[16,8448]{1,0:T(8,128)(2,1)S(1)}, u32[]{:S(2)}, u32[]{:S(2)}) collective-permute-start(bf16[16,8448]{1,0:T(8,128)(2,1)S(1)} %collective-permute-done.5.refs_7_), channel_id=1, source_target_pairs={{0,192},{8,200},{16,208},{24,216},{32,224},{40,232},{48,240},{56,2... | collective-permute-start | bytes 811016 | tf_op jit(solution)/shard_map/ppermute | solution.py:119
  31.2 2.3 %collective-permute-start.28 = (bf16[16,8448]{1,0:T(8,128)(2,1)S(1)}, bf16[16,8448]{1,0:T(8,128)(2,1)S(1)}, u32[]{:S(2)}, u32[]{:S(2)}) collective-permute-start(bf16[16,8448]{1,0:T(8,128)(2,1)S(1)} %collective-permute-done.24.refs_8_), channel_id=1, source_target_pairs={{0,56},{8,0},{16,8},{24,16},{32,24},{40,32},{48,40},{56,48},{64,12... | collective-permute-start | bytes 811016 | tf_op jit(solution)/shard_map/ppermute | solution.py:119
  35.0 2.5 %collective-permute-start.2 = (bf16[16,8448]{1,0:T(8,128)(2,1)S(1)}, bf16[16,8448]{1,0:T(8,128)(2,1)}, u32[]{:S(2)}, u32[]{:S(2)}) collective-permute-start(bf16[16,8448]{1,0:T(8,128)(2,1)S(1)} %collective-permute-done.1.refs_10_), channel_id=1, source_target_pairs={{0,56},{8,0},{16,8},{24,16},{32,24},{40,32},{48,40},{56,48},{64,12... | collective-permute-start | bytes 811016 | tf_op jit(solution)/shard_map/ppermute | solution.py:119
  37.5 4.1 %collective-permute-done.30.refs_17_ = bf16[16,8448]{1,0:T(8,128)(2,1)S(1)} collective-permute-done((bf16[16,8448]{1,0:T(8,128)(2,1)S(1)}, bf16[16,8448]{1,0:T(8,128)(2,1)S(1)}, u32[]{:S(2)}, u32[]{:S(2)}) %collective-permute-start.30) | collective-permute-done | bytes 270368 | tf_op jit(solution)/shard_map/ppermute | solution.py:119
  44.8 2.5 %collective-permute-start.10 = (bf16[16,8448]{1,0:T(8,128)(2,1)S(1)}, bf16[16,8448]{1,0:T(8,128)(2,1)S(1)}, u32[]{:S(2)}, u32[]{:S(2)}) collective-permute-start(bf16[16,8448]{1,0:T(8,128)(2,1)S(1)} %collective-permute-done.9.refs_16_), channel_id=1, source_target_pairs={{0,56},{8,0},{16,8},{24,16},{32,24},{40,32},{48,40},{56,48},{64,12... | collective-permute-start | bytes 811016 | tf_op jit(solution)/shard_map/ppermute | solution.py:119
  47.3 1.2 %collective-permute-start.21 = (bf16[16,8448]{1,0:T(8,128)(2,1)S(1)}, bf16[16,8448]{1,0:T(8,128)(2,1)}, u32[]{:S(2)}, u32[]{:S(2)}) collective-permute-start(bf16[16,8448]{1,0:T(8,128)(2,1)S(1)} %collective-permute-done.9.refs_16_), channel_id=1, source_target_pairs={{0,64},{8,72},{16,80},{24,88},{32,96},{40,104},{48,112},{56,120},{... | collective-permute-start | bytes 811016 | tf_op jit(solution)/shard_map/ppermute | solution.py:119
  48.5 1.5 %collective-permute-start.20 = (bf16[16,8448]{1,0:T(8,128)(2,1)S(1)}, bf16[16,8448]{1,0:T(8,128)(2,1)}, u32[]{:S(2)}, u32[]{:S(2)}) collective-permute-start(bf16[16,8448]{1,0:T(8,128)(2,1)S(1)} %collective-permute-done.6.refs_13_), channel_id=1, source_target_pairs={{0,192},{8,200},{16,208},{24,216},{32,224},{40,232},{48,240},{56,2... | collective-permute-start | bytes 811016 | tf_op jit(solution)/shard_map/ppermute | solution.py:119
  50.7 1.4 %collective-permute-start.12 = (bf16[16,8448]{1,0:T(8,128)(2,1)}, bf16[16,8448]{1,0:T(8,128)(2,1)}, u32[]{:S(2)}, u32[]{:S(2)}) collective-permute-start(bf16[16,8448]{1,0:T(8,128)(2,1)} %collective-permute-done.2.refs_2_), channel_id=1, source_target_pairs={{0,192},{8,200},{16,208},{24,216},{32,224},{40,232},{48,240},{56,2... | collective-permute-start | bytes 811016 | tf_op jit(solution)/shard_map/ppermute | solution.py:119
  52.1 1.2 %collective-permute-done.7.refs_3_ = bf16[16,8448]{1,0:T(8,128)(2,1)} collective-permute-done((bf16[16,8448]{1,0:T(8,128)(2,1)S(1)}, bf16[16,8448]{1,0:T(8,128)(2,1)}, u32[]{:S(2)}, u32[]{:S(2)}) %collective-permute-start.7) | collective-permute-done | bytes 270368 | tf_op jit(solution)/shard_map/ppermute | solution.py:119
  53.9 2.4 %collective-permute-start.14 = (bf16[16,8448]{1,0:T(8,128)(2,1)}, bf16[16,8448]{1,0:T(8,128)(2,1)}, u32[]{:S(2)}, u32[]{:S(2)}) collective-permute-start(bf16[16,8448]{1,0:T(8,128)(2,1)} %collective-permute-done.7.refs_3_), channel_id=1, source_target_pairs={{0,192},{8,200},{16,208},{24,216},{32,224},{40,232},{48,240},{56,2... | collective-permute-start | bytes 811016 | tf_op jit(solution)/shard_map/ppermute | solution.py:119
  59.8 4.3 %collective-permute-done.14.refs_9_ = bf16[16,8448]{1,0:T(8,128)(2,1)} collective-permute-done((bf16[16,8448]{1,0:T(8,128)(2,1)}, bf16[16,8448]{1,0:T(8,128)(2,1)}, u32[]{:S(2)}, u32[]{:S(2)}) %collective-permute-start.14) | collective-permute-done | bytes 270368 | tf_op jit(solution)/shard_map/ppermute | solution.py:119
  64.1 2.2 %copy-done = bf16[1,512,4096]{2,1,0:T(8,128)(2,1)S(1)} copy-done((bf16[1,512,4096]{2,1,0:T(8,128)(2,1)S(1)}, bf16[1,512,4096]{2,1,0:T(8,128)(2,1)}, u32[]{:S(2)}) %copy-start) | copy-done | bytes 4194328
  66.3 2.2 %copy-done.1 = bf16[1,512,4096]{2,1,0:T(8,128)(2,1)S(1)} copy-done((bf16[1,512,4096]{2,1,0:T(8,128)(2,1)S(1)}, bf16[1,512,4096]{2,1,0:T(8,128)(2,1)}, u32[]{:S(2)}) %copy-start.1) | copy-done | bytes 4194328
  71.4 2.6 %shard_map.55.refs_10_ = f32[512,256]{1,0:T(8,128)S(1)} custom-call(bf16[512,4096]{1,0:T(8,128)(2,1)S(1)} %bitcast.13, bf16[512,4096]{1,0:T(8,128)(2,1)S(1)} %bitcast.16, bf16[16,8448]{1,0:T(8,128)(2,1)S(1)} %pad_maximum_fusion.refs_2_, bf16[16,8448]{1,0:T(8,128)(2,1)S(1)} %collective-permute-done.4.refs_3_, ...), custom_call_target="tpu_custom_call" | custom-call | flops 2147483648 | tf_op jit(solution)/shard_map/pallas_call | solution.py:98
  74.0 3.8 %shard_map.56.refs_10_ = f32[512,256]{1,0:T(8,128)S(1)} custom-call(bf16[512,4096]{1,0:T(8,128)(2,1)S(1)} %bitcast.14, bf16[512,4096]{1,0:T(8,128)(2,1)S(1)} %bitcast.17, bf16[16,8448]{1,0:T(8,128)(2,1)} %collective-permute-done.2.refs_2_, bf16[16,8448]{1,0:T(8,128)(2,1)} %collective-permute-done.7.refs_3_, bf16[16,8448]{1,0:T(8,128)(2,1)S(1)} %copy-done.13, ...), custom_call_target="tpu_custom_call" | custom-call | flops 1073741824 | tf_op jit(solution)/shard_map/pallas_call | solution.py:98
  77.9 3.5 %shard_map.57 = f32[512,256]{1,0:T(8,128)S(1)} custom-call(bf16[512,4096]{1,0:T(8,128)(2,1)S(1)} %bitcast.15, bf16[512,4096]{1,0:T(8,128)(2,1)S(1)} %bitcast.18, bf16[16,8448]{1,0:T(8,128)(2,1)} %collective-permute-done.3.refs_2_, bf16[16,8448]{1,0:T(8,128)(2,1)S(1)} %collective-permute-done.8.refs_3_, bf16[16,8448]{1,0:T(8,128)(2,1)S(1)} %collective-permute-done.11.refs_4_, ...), custom_call_target="tpu_custom_call" | custom-call | flops 1073741824 | tf_op jit(solution)/shard_map/pallas_call | solution.py:98
  81.5 5.8 %collective-permute-start.31 = (f32[2,128,256]{2,1,0:T(8,128)S(1)}, f32[2,128,256]{2,1,0:T(8,128)S(1)}, u32[]{:S(2)}, u32[]{:S(2)}) collective-permute-start(f32[2,128,256]{2,1,0:T(8,128)S(1)} %dynamic-slice_bitcast_fusion), channel_id=1, source_target_pairs={{0,1},{1,0},{2,3},{3,2},{4,5},{5,4},{6,7},{7,6},{8,9},{9,8},{10,11... | collective-permute-start | bytes 786440 | tf_op jit(solution)/shard_map/ppermute | solution.py:132
  88.5 1.4 %collective-permute-start.32 = (f32[128,256]{1,0:T(8,128)S(1)}, f32[128,256]{1,0:T(8,128)S(1)}, u32[]{:S(2)}, u32[]{:S(2)}) collective-permute-start(f32[128,256]{1,0:T(8,128)S(1)} %get-tuple-element.5), channel_id=1, source_target_pairs={{0,4},{1,5},{2,6},{3,7},{4,0},{5,1},{6,2},{7,3},{8,12},{9,13},{10,... | collective-permute-start | bytes 393224 | tf_op jit(solution)/shard_map/ppermute | solution.py:142
  89.9 1.9 %collective-permute-start.33 = (f32[128,256]{1,0:T(8,128)S(1)}, f32[128,256]{1,0:T(8,128)S(1)}, u32[]{:S(2)}, u32[]{:S(2)}) collective-permute-start(f32[128,256]{1,0:T(8,128)S(1)} %get-tuple-element.6), channel_id=1, source_target_pairs={{0,6},{1,7},{2,4},{3,5},{4,2},{5,3},{6,0},{7,1},{8,14},{9,15},{10,... | collective-permute-start | bytes 393224 | tf_op jit(solution)/shard_map/ppermute | solution.py:142
  93.2 3.4 %collective-permute-done.33 = f32[128,256]{1,0:T(8,128)S(1)} collective-permute-done((f32[128,256]{1,0:T(8,128)S(1)}, f32[128,256]{1,0:T(8,128)S(1)}, u32[]{:S(2)}, u32[]{:S(2)}) %collective-permute-start.33) | collective-permute-done | bytes 131104 | tf_op jit(solution)/shard_map/ppermute | solution.py:142
  96.6 1.9 %collective-permute-done.34 = f32[128,256]{1,0:T(8,128)S(1)} collective-permute-done((f32[128,256]{1,0:T(8,128)S(1)}, f32[128,256]{1,0:T(8,128)S(1)}, u32[]{:S(2)}, u32[]{:S(2)}) %collective-permute-start.34) | collective-permute-done | bytes 131104 | tf_op jit(solution)/shard_map/ppermute | solution.py:142
  (78 shorter events, 17.8 us)
Async XLA Ops:
  1.0 11.6 %collective-permute-start = (bf16[16,8448]{1,0:T(8,128)(2,1)S(1)}, bf16[16,8448]{1,0:T(8,128)(2,1)S(1)}, u32[]{:S(2)}, u32[]{:S(2)}) collective-permute-start(bf16[16,8448]{1,0:T(8,128)(2,1)S(1)} %pad_maximum_fusion.refs_2_), channel_id=1, source_target_pairs={{0,56},{8,0},{16,8},{24,16},{32,24},{40,32},{48,40},{56,48},{64,12... | collective-permute-start | bytes 811016 | tf_op jit(solution)/shard_map/ppermute | solution.py:119
  7.5 8.6 %collective-permute-start.4 = (bf16[16,8448]{1,0:T(8,128)(2,1)S(1)}, bf16[16,8448]{1,0:T(8,128)(2,1)S(1)}, u32[]{:S(2)}, u32[]{:S(2)}) collective-permute-start(bf16[16,8448]{1,0:T(8,128)(2,1)S(1)} %pad_maximum_fusion.refs_2_), channel_id=1, source_target_pairs={{0,8},{8,16},{16,24},{24,32},{32,40},{40,48},{48,56},{56,0},{64,72... | collective-permute-start | bytes 811016 | tf_op jit(solution)/shard_map/ppermute | solution.py:119
  7.5 8.6 %collective-permute-start.22 = (bf16[16,8448]{1,0:T(8,128)(2,1)S(1)}, bf16[16,8448]{1,0:T(8,128)(2,1)S(1)}, u32[]{:S(2)}, u32[]{:S(2)}) collective-permute-start(bf16[16,8448]{1,0:T(8,128)(2,1)S(1)} %pad_maximum_fusion.refs_2_), channel_id=1, source_target_pairs={{0,64},{8,72},{16,80},{24,88},{32,96},{40,104},{48,112},{56,120},{... | collective-permute-start | bytes 811016 | tf_op jit(solution)/shard_map/ppermute | solution.py:119
  8.7 9.9 %collective-permute-start.23 = (bf16[16,8448]{1,0:T(8,128)(2,1)S(1)}, bf16[16,8448]{1,0:T(8,128)(2,1)S(1)}, u32[]{:S(2)}, u32[]{:S(2)}) collective-permute-start(bf16[16,8448]{1,0:T(8,128)(2,1)S(1)} %pad_maximum_fusion.refs_2_), channel_id=1, source_target_pairs={{0,192},{8,200},{16,208},{24,216},{32,224},{40,232},{48,240},{56,2... | collective-permute-start | bytes 811016 | tf_op jit(solution)/shard_map/ppermute | solution.py:119
  12.6 7.7 %collective-permute-start.1 = (bf16[16,8448]{1,0:T(8,128)(2,1)S(1)}, bf16[16,8448]{1,0:T(8,128)(2,1)S(1)}, u32[]{:S(2)}, u32[]{:S(2)}) collective-permute-start(bf16[16,8448]{1,0:T(8,128)(2,1)S(1)} %collective-permute-done.refs_6_), channel_id=1, source_target_pairs={{0,56},{8,0},{16,8},{24,16},{32,24},{40,32},{48,40},{56,48},{64,12... | collective-permute-start | bytes 811016 | tf_op jit(solution)/shard_map/ppermute | solution.py:119
  16.1 7.4 %collective-permute-start.5 = (bf16[16,8448]{1,0:T(8,128)(2,1)S(1)}, bf16[16,8448]{1,0:T(8,128)(2,1)S(1)}, u32[]{:S(2)}, u32[]{:S(2)}) collective-permute-start(bf16[16,8448]{1,0:T(8,128)(2,1)S(1)} %collective-permute-done.4.refs_3_), channel_id=1, source_target_pairs={{0,8},{8,16},{16,24},{24,32},{32,40},{40,48},{48,56},{56,0},{64,72... | collective-permute-start | bytes 811016 | tf_op jit(solution)/shard_map/ppermute | solution.py:119
  16.1 9.9 %collective-permute-start.24 = (bf16[16,8448]{1,0:T(8,128)(2,1)S(1)}, bf16[16,8448]{1,0:T(8,128)(2,1)S(1)}, u32[]{:S(2)}, u32[]{:S(2)}) collective-permute-start(bf16[16,8448]{1,0:T(8,128)(2,1)S(1)} %collective-permute-done.22.refs_4_), channel_id=1, source_target_pairs={{0,64},{8,72},{16,80},{24,88},{32,96},{40,104},{48,112},{56,120},{... | collective-permute-start | bytes 811016 | tf_op jit(solution)/shard_map/ppermute | solution.py:119
  17.4 12.0 %collective-permute-start.27 = (bf16[16,8448]{1,0:T(8,128)(2,1)S(1)}, bf16[16,8448]{1,0:T(8,128)(2,1)S(1)}, u32[]{:S(2)}, u32[]{:S(2)}) collective-permute-start(bf16[16,8448]{1,0:T(8,128)(2,1)S(1)} %collective-permute-done.refs_6_), channel_id=1, source_target_pairs={{0,64},{8,72},{16,80},{24,88},{32,96},{40,104},{48,112},{56,120},{... | collective-permute-start | bytes 811016 | tf_op jit(solution)/shard_map/ppermute | solution.py:119
  18.6 12.1 %collective-permute-start.25 = (bf16[16,8448]{1,0:T(8,128)(2,1)S(1)}, bf16[16,8448]{1,0:T(8,128)(2,1)S(1)}, u32[]{:S(2)}, u32[]{:S(2)}) collective-permute-start(bf16[16,8448]{1,0:T(8,128)(2,1)S(1)} %collective-permute-done.4.refs_3_), channel_id=1, source_target_pairs={{0,192},{8,200},{16,208},{24,216},{32,224},{40,232},{48,240},{56,2... | collective-permute-start | bytes 811016 | tf_op jit(solution)/shard_map/ppermute | solution.py:119
  20.4 10.8 %collective-permute-start.26 = (bf16[16,8448]{1,0:T(8,128)(2,1)S(1)}, bf16[16,8448]{1,0:T(8,128)(2,1)S(1)}, u32[]{:S(2)}, u32[]{:S(2)}) collective-permute-start(bf16[16,8448]{1,0:T(8,128)(2,1)S(1)} %collective-permute-done.22.refs_4_), channel_id=1, source_target_pairs={{0,8},{8,16},{16,24},{24,32},{32,40},{40,48},{48,56},{56,0},{64,72... | collective-permute-start | bytes 811016 | tf_op jit(solution)/shard_map/ppermute | solution.py:119
  23.5 10.0 %collective-permute-start.18 = (bf16[16,8448]{1,0:T(8,128)(2,1)S(1)}, bf16[16,8448]{1,0:T(8,128)(2,1)S(1)}, u32[]{:S(2)}, u32[]{:S(2)}) collective-permute-start(bf16[16,8448]{1,0:T(8,128)(2,1)S(1)} %collective-permute-done.refs_6_), channel_id=1, source_target_pairs={{0,192},{8,200},{16,208},{24,216},{32,224},{40,232},{48,240},{56,2... | collective-permute-start | bytes 811016 | tf_op jit(solution)/shard_map/ppermute | solution.py:119
  26.0 9.1 %collective-permute-start.9 = (bf16[16,8448]{1,0:T(8,128)(2,1)S(1)}, bf16[16,8448]{1,0:T(8,128)(2,1)S(1)}, u32[]{:S(2)}, u32[]{:S(2)}) collective-permute-start(bf16[16,8448]{1,0:T(8,128)(2,1)S(1)} %collective-permute-done.1.refs_10_), channel_id=1, source_target_pairs={{0,64},{8,72},{16,80},{24,88},{32,96},{40,104},{48,112},{56,120},{... | collective-permute-start | bytes 811016 | tf_op jit(solution)/shard_map/ppermute | solution.py:119
  29.4 8.1 %collective-permute-start.6 = (bf16[16,8448]{1,0:T(8,128)(2,1)S(1)}, bf16[16,8448]{1,0:T(8,128)(2,1)S(1)}, u32[]{:S(2)}, u32[]{:S(2)}) collective-permute-start(bf16[16,8448]{1,0:T(8,128)(2,1)S(1)} %collective-permute-done.5.refs_7_), channel_id=1, source_target_pairs={{0,192},{8,200},{16,208},{24,216},{32,224},{40,232},{48,240},{56,2... | collective-permute-start | bytes 811016 | tf_op jit(solution)/shard_map/ppermute | solution.py:119
  30.7 10.9 %collective-permute-start.30 = (bf16[16,8448]{1,0:T(8,128)(2,1)S(1)}, bf16[16,8448]{1,0:T(8,128)(2,1)S(1)}, u32[]{:S(2)}, u32[]{:S(2)}) collective-permute-start(bf16[16,8448]{1,0:T(8,128)(2,1)S(1)} %collective-permute-done.1.refs_10_), channel_id=1, source_target_pairs={{0,192},{8,200},{16,208},{24,216},{32,224},{40,232},{48,240},{56,2... | collective-permute-start | bytes 811016 | tf_op jit(solution)/shard_map/ppermute | solution.py:119
  31.2 12.0 %collective-permute-start.28 = (bf16[16,8448]{1,0:T(8,128)(2,1)S(1)}, bf16[16,8448]{1,0:T(8,128)(2,1)S(1)}, u32[]{:S(2)}, u32[]{:S(2)}) collective-permute-start(bf16[16,8448]{1,0:T(8,128)(2,1)S(1)} %collective-permute-done.24.refs_8_), channel_id=1, source_target_pairs={{0,56},{8,0},{16,8},{24,16},{32,24},{40,32},{48,40},{56,48},{64,12... | collective-permute-start | bytes 811016 | tf_op jit(solution)/shard_map/ppermute | solution.py:119
  34.2 9.9 %collective-permute-start.29 = (bf16[16,8448]{1,0:T(8,128)(2,1)S(1)}, bf16[16,8448]{1,0:T(8,128)(2,1)S(1)}, u32[]{:S(2)}, u32[]{:S(2)}) collective-permute-start(bf16[16,8448]{1,0:T(8,128)(2,1)S(1)} %collective-permute-done.24.refs_8_), channel_id=1, source_target_pairs={{0,8},{8,16},{16,24},{24,32},{32,40},{40,48},{48,56},{56,0},{64,72... | collective-permute-start | bytes 811016 | tf_op jit(solution)/shard_map/ppermute | solution.py:119
  35.0 12.3 %collective-permute-start.2 = (bf16[16,8448]{1,0:T(8,128)(2,1)S(1)}, bf16[16,8448]{1,0:T(8,128)(2,1)}, u32[]{:S(2)}, u32[]{:S(2)}) collective-permute-start(bf16[16,8448]{1,0:T(8,128)(2,1)S(1)} %collective-permute-done.1.refs_10_), channel_id=1, source_target_pairs={{0,56},{8,0},{16,8},{24,16},{32,24},{40,32},{48,40},{56,48},{64,12... | collective-permute-start | bytes 811016 | tf_op jit(solution)/shard_map/ppermute | solution.py:119
  37.5 11.1 %collective-permute-start.16 = (bf16[16,8448]{1,0:T(8,128)(2,1)S(1)}, bf16[16,8448]{1,0:T(8,128)(2,1)S(1)}, u32[]{:S(2)}, u32[]{:S(2)}) collective-permute-start(bf16[16,8448]{1,0:T(8,128)(2,1)S(1)} %collective-permute-done.5.refs_7_), channel_id=1, source_target_pairs={{0,8},{8,16},{16,24},{24,32},{32,40},{40,48},{48,56},{56,0},{64,72... | collective-permute-start | bytes 811016 | tf_op jit(solution)/shard_map/ppermute | solution.py:119
  42.3 7.8 %collective-permute-start.19 = (bf16[16,8448]{1,0:T(8,128)(2,1)S(1)}, bf16[16,8448]{1,0:T(8,128)(2,1)S(1)}, u32[]{:S(2)}, u32[]{:S(2)}) collective-permute-start(bf16[16,8448]{1,0:T(8,128)(2,1)S(1)} %collective-permute-done.5.refs_7_), channel_id=1, source_target_pairs={{0,64},{8,72},{16,80},{24,88},{32,96},{40,104},{48,112},{56,120},{... | collective-permute-start | bytes 811016 | tf_op jit(solution)/shard_map/ppermute | solution.py:119
  43.9 9.4 %collective-permute-start.7 = (bf16[16,8448]{1,0:T(8,128)(2,1)S(1)}, bf16[16,8448]{1,0:T(8,128)(2,1)}, u32[]{:S(2)}, u32[]{:S(2)}) collective-permute-start(bf16[16,8448]{1,0:T(8,128)(2,1)S(1)} %collective-permute-done.6.refs_13_), channel_id=1, source_target_pairs={{0,8},{8,16},{16,24},{24,32},{32,40},{40,48},{48,56},{56,0},{64,72... | collective-permute-start | bytes 811016 | tf_op jit(solution)/shard_map/ppermute | solution.py:119
  44.8 9.0 %collective-permute-start.10 = (bf16[16,8448]{1,0:T(8,128)(2,1)S(1)}, bf16[16,8448]{1,0:T(8,128)(2,1)S(1)}, u32[]{:S(2)}, u32[]{:S(2)}) collective-permute-start(bf16[16,8448]{1,0:T(8,128)(2,1)S(1)} %collective-permute-done.9.refs_16_), channel_id=1, source_target_pairs={{0,56},{8,0},{16,8},{24,16},{32,24},{40,32},{48,40},{56,48},{64,12... | collective-permute-start | bytes 811016 | tf_op jit(solution)/shard_map/ppermute | solution.py:119
  47.3 9.7 %collective-permute-start.21 = (bf16[16,8448]{1,0:T(8,128)(2,1)S(1)}, bf16[16,8448]{1,0:T(8,128)(2,1)}, u32[]{:S(2)}, u32[]{:S(2)}) collective-permute-start(bf16[16,8448]{1,0:T(8,128)(2,1)S(1)} %collective-permute-done.9.refs_16_), channel_id=1, source_target_pairs={{0,64},{8,72},{16,80},{24,88},{32,96},{40,104},{48,112},{56,120},{... | collective-permute-start | bytes 811016 | tf_op jit(solution)/shard_map/ppermute | solution.py:119
  48.5 8.5 %collective-permute-start.20 = (bf16[16,8448]{1,0:T(8,128)(2,1)S(1)}, bf16[16,8448]{1,0:T(8,128)(2,1)}, u32[]{:S(2)}, u32[]{:S(2)}) collective-permute-start(bf16[16,8448]{1,0:T(8,128)(2,1)S(1)} %collective-permute-done.6.refs_13_), channel_id=1, source_target_pairs={{0,192},{8,200},{16,208},{24,216},{32,224},{40,232},{48,240},{56,2... | collective-permute-start | bytes 811016 | tf_op jit(solution)/shard_map/ppermute | solution.py:119
  50.7 7.6 %collective-permute-start.12 = (bf16[16,8448]{1,0:T(8,128)(2,1)}, bf16[16,8448]{1,0:T(8,128)(2,1)}, u32[]{:S(2)}, u32[]{:S(2)}) collective-permute-start(bf16[16,8448]{1,0:T(8,128)(2,1)} %collective-permute-done.2.refs_2_), channel_id=1, source_target_pairs={{0,192},{8,200},{16,208},{24,216},{32,224},{40,232},{48,240},{56,2... | collective-permute-start | bytes 811016 | tf_op jit(solution)/shard_map/ppermute | solution.py:119
  53.9 10.3 %collective-permute-start.14 = (bf16[16,8448]{1,0:T(8,128)(2,1)}, bf16[16,8448]{1,0:T(8,128)(2,1)}, u32[]{:S(2)}, u32[]{:S(2)}) collective-permute-start(bf16[16,8448]{1,0:T(8,128)(2,1)} %collective-permute-done.7.refs_3_), channel_id=1, source_target_pairs={{0,192},{8,200},{16,208},{24,216},{32,224},{40,232},{48,240},{56,2... | collective-permute-start | bytes 811016 | tf_op jit(solution)/shard_map/ppermute | solution.py:119
  57.0 20.8 %collective-permute-start.17 = (bf16[16,8448]{1,0:T(8,128)(2,1)}, bf16[16,8448]{1,0:T(8,128)(2,1)S(1)}, u32[]{:S(2)}, u32[]{:S(2)}) collective-permute-start(bf16[16,8448]{1,0:T(8,128)(2,1)} %copy-done.10), channel_id=1, source_target_pairs={{0,64},{8,72},{16,80},{24,88},{32,96},{40,104},{48,112},{56,120},{... | collective-permute-start | bytes 811016 | tf_op jit(solution)/shard_map/ppermute | solution.py:119
  57.0 20.8 %collective-permute-start.11 = (bf16[16,8448]{1,0:T(8,128)(2,1)}, bf16[16,8448]{1,0:T(8,128)(2,1)S(1)}, u32[]{:S(2)}, u32[]{:S(2)}) collective-permute-start(bf16[16,8448]{1,0:T(8,128)(2,1)} %copy-done.14), channel_id=1, source_target_pairs={{0,64},{8,72},{16,80},{24,88},{32,96},{40,104},{48,112},{56,120},{... | collective-permute-start | bytes 811016 | tf_op jit(solution)/shard_map/ppermute | solution.py:119
  58.3 19.5 %collective-permute-start.13 = (bf16[16,8448]{1,0:T(8,128)(2,1)}, bf16[16,8448]{1,0:T(8,128)(2,1)S(1)}, u32[]{:S(2)}, u32[]{:S(2)}) collective-permute-start(bf16[16,8448]{1,0:T(8,128)(2,1)} %copy-done.14), channel_id=1, source_target_pairs={{0,56},{8,0},{16,8},{24,16},{32,24},{40,32},{48,40},{56,48},{64,12... | collective-permute-start | bytes 811016 | tf_op jit(solution)/shard_map/ppermute | solution.py:119
  59.2 18.7 %collective-permute-start.8 = (bf16[16,8448]{1,0:T(8,128)(2,1)}, bf16[16,8448]{1,0:T(8,128)(2,1)S(1)}, u32[]{:S(2)}, u32[]{:S(2)}) collective-permute-start(bf16[16,8448]{1,0:T(8,128)(2,1)} %collective-permute-done.7.refs_3_), channel_id=1, source_target_pairs={{0,8},{8,16},{16,24},{24,32},{32,40},{40,48},{48,56},{56,0},{64,72... | collective-permute-start | bytes 811016 | tf_op jit(solution)/shard_map/ppermute | solution.py:119
  64.1 13.7 %collective-permute-start.15 = (bf16[16,8448]{1,0:T(8,128)(2,1)}, bf16[16,8448]{1,0:T(8,128)(2,1)S(1)}, u32[]{:S(2)}, u32[]{:S(2)}) collective-permute-start(bf16[16,8448]{1,0:T(8,128)(2,1)} %collective-permute-done.14.refs_9_), channel_id=1, source_target_pairs={{0,8},{8,16},{16,24},{24,32},{32,40},{40,48},{48,56},{56,0},{64,72... | collective-permute-start | bytes 811016 | tf_op jit(solution)/shard_map/ppermute | solution.py:119
  81.5 6.9 %collective-permute-start.31 = (f32[2,128,256]{2,1,0:T(8,128)S(1)}, f32[2,128,256]{2,1,0:T(8,128)S(1)}, u32[]{:S(2)}, u32[]{:S(2)}) collective-permute-start(f32[2,128,256]{2,1,0:T(8,128)S(1)} %dynamic-slice_bitcast_fusion), channel_id=1, source_target_pairs={{0,1},{1,0},{2,3},{3,2},{4,5},{5,4},{6,7},{7,6},{8,9},{9,8},{10,11... | collective-permute-start | bytes 786440 | tf_op jit(solution)/shard_map/ppermute | solution.py:132
  89.9 6.8 %collective-permute-start.33 = (f32[128,256]{1,0:T(8,128)S(1)}, f32[128,256]{1,0:T(8,128)S(1)}, u32[]{:S(2)}, u32[]{:S(2)}) collective-permute-start(f32[128,256]{1,0:T(8,128)S(1)} %get-tuple-element.6), channel_id=1, source_target_pairs={{0,6},{1,7},{2,4},{3,5},{4,2},{5,3},{6,0},{7,1},{8,14},{9,15},{10,... | collective-permute-start | bytes 393224 | tf_op jit(solution)/shard_map/ppermute | solution.py:142
  (19 other events, 47.6 us)

commit v3 on v2

v3 whole, which is shorter than its diff:
```python
import functools

import jax
import jax.numpy as jnp
from jax import lax
from jax.experimental import pallas as pl
from jax.experimental.pallas import tpu as pltpu
from jax.sharding import PartitionSpec as P


LAYERS = 4
ACROSS, ALONG = 4, 8
HOPS = {"zp": (0, 1), "zm": (0, -1), "xp": (1, 0), "xm": (-1, 0)}
ROUTE = (
    ("zm", (0, 0)),
    ("zp", (0, 0)),
    ("xm", (0, 0)),
    ("xp", (0, 0)),
    ("zm", (0, 7)),
    ("zp", (0, 1)),
    ("xp", (0, 1)),
    ("xm", (3, 0)),
    ("zm", (3, 0)),
    ("xm", (0, 1)),
    ("xp", (0, 6)),
    ("zm", (0, 6)),
    ("zp", (0, 2)),
    ("zp", (1, 1)),
    ("xp", (1, 1)),
    ("xm", (0, 6)),
    ("zm", (1, 6)),
    ("xm", (0, 2)),
    ("xp", (1, 6)),
    ("xp", (0, 7)),
    ("xp", (0, 3)),
    ("xm", (0, 3)),
    ("zm", (0, 5)),
    ("zp", (2, 1)),
    ("zm", (1, 5)),
    ("zm", (2, 6)),
    ("zp", (2, 6)),
    ("xm", (0, 5)),
    ("zp", (3, 3)),
    ("xm", (3, 3)),
    ("xp", (1, 4)),
)
CHUNKS = (16, 16)
TOUCH_AFTER = (4, 10, 16, 22, 31)


def hop_pairs(hop):
    dx, dz = HOPS[hop]
    return [
        (x * ALONG + z, (x + dx) % ACROSS * ALONG + (z + dz) % ALONG)
        for x in range(ACROSS)
        for z in range(ALONG)
    ]


def moved(offset, hop):
    dx, dz = HOPS[hop]
    return ((offset[0] + dx) % ACROSS, (offset[1] + dz) % ALONG)


STEP = 1024


def contract(left, right):
    return lax.dot_general(
        left, right, (((1,), (1,)), ((), ())), preferred_element_type=jnp.float32
    )


def chunk_kernel(count, width, inverse_width, first, tag, *refs):
    residents = refs[:2]
    blocks = refs[2 : 2 + count]
    rest = refs[2 + count :]

    def columns(begin, end):
        return jnp.concatenate([block[:, begin:end] for block in blocks], axis=0)

    grams = []
    for tensor, resident in enumerate(residents):
        gram = None
        for begin in range(0, width, STEP):
            base = tensor * width + begin
            piece = contract(resident[:, begin : begin + STEP], columns(base, base + STEP))
            gram = piece if gram is None else gram + piece
        grams.append(gram)
    kernel = (grams[0] * grams[1] * inverse_width).astype(jnp.bfloat16)
    rows = columns(2 * width, blocks[0].shape[1])
    part = jnp.dot(kernel, rows, preferred_element_type=jnp.float32)
    if first:
        rest[0][...] = part
    else:
        rest[1][...] = rest[0][...] + part


def touch_kernel(act, grad, *refs):
    out = refs[-1]
    out[...] = act[:16, :128] + grad[:16, :128]


def touch(act, grad, tag):
    in_vmem = pl.BlockSpec(memory_space=pltpu.VMEM)
    operands = [act, grad] + ([] if tag is None else [tag])
    return pl.pallas_call(
        touch_kernel,
        out_shape=jax.ShapeDtypeStruct((16, 128), act.dtype),
        in_specs=[in_vmem] * len(operands),
        out_specs=in_vmem,
        compiler_params=pltpu.CompilerParams(vmem_limit_bytes=1 << 20),
        cost_estimate=pl.CostEstimate(flops=1, bytes_accessed=1, transcendentals=0),
    )(*operands)


def add_chunk(total, tag, res_act, res_grad, blocks):
    width = res_act.shape[1]
    first = total is None
    operands = [tag, res_act, res_grad, *blocks] + ([] if first else [total])
    _, wide = blocks[0].shape
    out = jax.ShapeDtypeStruct((res_act.shape[0], wide - 2 * width), jnp.float32)
    return pl.pallas_call(
        functools.partial(chunk_kernel, len(blocks), width, 1.0 / width, first),
        out_shape=out,
        in_specs=[pl.BlockSpec(memory_space=pltpu.VMEM)] * len(operands),
        out_specs=pl.BlockSpec(memory_space=pltpu.VMEM),
        compiler_params=pltpu.CompilerParams(vmem_limit_bytes=4 << 20),
        cost_estimate=pl.CostEstimate(flops=1, bytes_accessed=1, transcendentals=0),
    )(*operands)


def on_device(resident_act, resident_grad, source_act, source_grad, probes):
    blocks = lax.axis_size("blk")
    source_total = source_act.shape[1] * blocks * lax.axis_size("src")
    res_act, res_grad = resident_act[0], resident_grad[0]

    own = jnp.concatenate([source_act[0], source_grad[0], probes], axis=1)
    tags = [None]
    for _ in range(len(TOUCH_AFTER)):
        tags.append(touch(res_act, res_grad, tags[-1]))
    held = {(0, 0): own}
    order = [(0, 0)]
    for hop, offset in ROUTE:
        there = moved(offset, hop)
        held[there] = lax.ppermute(held[offset], "blk", hop_pairs(hop))
        order.append(there)
    total = None
    begin = 0
    for index, size in enumerate(CHUNKS):
        total = add_chunk(total, tags[-1] if index == len(CHUNKS) - 1 else tags[1], res_act, res_grad, [held[o] for o in order[begin : begin + size]])
        begin += size

    layer = lax.axis_index("layer")
    core, high = layer % 2, layer // 2
    pieces = total.reshape(2, 2, -1, total.shape[1])
    keep = lax.dynamic_index_in_dim(pieces, core, 1, keepdims=False)
    give = lax.dynamic_index_in_dim(pieces, 1 - core, 1, keepdims=False)
    chip = keep + lax.ppermute(give, "layer", [(l, l ^ 1) for l in range(LAYERS)])
    mine = lax.dynamic_index_in_dim(chip, high, 0, keepdims=False)
    other = lax.dynamic_index_in_dim(chip, 1 - high, 0, keepdims=False).astype(jnp.bfloat16)

    def exchange(value, flip_src, flip_high):
        pairs = [
            (s * LAYERS + l, (s ^ flip_src) * LAYERS + (l ^ (2 * flip_high)))
            for s in range(2)
            for l in range(LAYERS)
        ]
        return lax.ppermute(value, ("src", "layer"), pairs)

    far = exchange(other, 0, 1)
    wrap = exchange(other, 1, 1)
    near = exchange(mine.astype(jnp.bfloat16), 1, 0)
    result = mine + near.astype(jnp.float32) + wrap.astype(jnp.float32) + far.astype(jnp.float32)
    return result * jnp.float32((LAYERS * source_total) ** (-0.5))


def solution(mesh):
    in_specs = (
        P("layer", "blk", None),
        P("layer", "blk", None),
        P("layer", ("blk", "src"), None),
        P("layer", ("blk", "src"), None),
        P(("blk", "src"), None),
    )
    out_specs = P(("blk", "layer"), None)
    return jax.shard_map(
        on_device, mesh=mesh, in_specs=in_specs, out_specs=out_specs, check_vma=False
    )
```

time: 99.5 us -> 99.9 us (level)
  the two profiles are of different devices: /device:TPU:1 before, /device:TPU:38 now
where the time goes in v3:
time: 99.9 us; the launch traced here: 99.5 us
  starting transfers between devices  51.8 us (52%)
  local copies, waits for them, and re-layouts  20.5 us (21%)
  waiting for transfers between devices  18.6 us (19%)
  Pallas kernels  6.69 us (7%)
  other arithmetic  1.72 us (2%)
    ppermute x31, starting transfers between devices, on_device(): held[there] = lax.ppermute(held[offset], 'blk', hop_pairs(hop))  47.1 us
    unnamed x52, local copies, waits for them, and re-layouts  20.4 us
    ppermute x31, waiting for transfers between devices, on_device(): held[there] = lax.ppermute(held[offset], 'blk', hop_pairs(hop))  12 us
    pallas_call x2, Pallas kernels, add_chunk(): pl.pallas_call(functools.partial(chunk_kernel, len(blocks), width, 1.0 /...  6.66 us
    ppermute x3, waiting for transfers between devices, exchange(): return lax.ppermute(value, ('src', 'layer'), pairs)  5.05 us
    ppermute x3, starting transfers between devices, exchange(): return lax.ppermute(value, ('src', 'layer'), pairs)  4.57 us
  transfers between devices with their start and end apart: 35, of which 10 were waited for; matrix products, arithmetic and copies ran while one was open for 0% of the time, Pallas kernels for 3%

profile of v3, /device:TPU:38, one launch (start us, length us, event | category | flops | bytes accessed | tf_op | source)
XLA Modules:
  0.0 99.5 jit_solution(14515482614803524051)
XLA Ops:
  1.0 2.0 %collective-permute-start.5 = (bf16[16,8448]{1,0:T(8,128)(2,1)S(1)}, bf16[16,8448]{1,0:T(8,128)(2,1)S(1)}, u32[]{:S(2)}, u32[]{:S(2)}) collective-permute-start(bf16[16,8448]{1,0:T(8,128)(2,1)S(1)} %pad_maximum_fusion.refs_2_), channel_id=1, source_target_pairs={{0,8},{8,16},{16,24},{24,32},{32,40},{40,48},{48,56},{56,0},{64,72... | collective-permute-start | bytes 811016 | tf_op jit(solution)/shard_map/ppermute | solution.py:146
  3.9 2.4 %collective-permute-start.26 = (bf16[16,8448]{1,0:T(8,128)(2,1)S(1)}, bf16[16,8448]{1,0:T(8,128)(2,1)S(1)}, u32[]{:S(2)}, u32[]{:S(2)}) collective-permute-start(bf16[16,8448]{1,0:T(8,128)(2,1)S(1)} %pad_maximum_fusion.refs_2_), channel_id=1, source_target_pairs={{0,64},{8,72},{16,80},{24,88},{32,96},{40,104},{48,112},{56,120},{... | collective-permute-start | bytes 811016 | tf_op jit(solution)/shard_map/ppermute | solution.py:146
  6.3 3.0 %collective-permute-done.5.refs_4_ = bf16[16,8448]{1,0:T(8,128)(2,1)S(1)} collective-permute-done((bf16[16,8448]{1,0:T(8,128)(2,1)S(1)}, bf16[16,8448]{1,0:T(8,128)(2,1)S(1)}, u32[]{:S(2)}, u32[]{:S(2)}) %collective-permute-start.5) | collective-permute-done | bytes 270368 | tf_op jit(solution)/shard_map/ppermute | solution.py:146
  9.3 1.9 %collective-permute-start.6 = (bf16[16,8448]{1,0:T(8,128)(2,1)S(1)}, bf16[16,8448]{1,0:T(8,128)(2,1)S(1)}, u32[]{:S(2)}, u32[]{:S(2)}) collective-permute-start(bf16[16,8448]{1,0:T(8,128)(2,1)S(1)} %collective-permute-done.5.refs_4_), channel_id=1, source_target_pairs={{0,8},{8,16},{16,24},{24,32},{32,40},{40,48},{48,56},{56,0},{64,72... | collective-permute-start | bytes 811016 | tf_op jit(solution)/shard_map/ppermute | solution.py:146
  11.2 2.3 %collective-permute-start.1 = (bf16[16,8448]{1,0:T(8,128)(2,1)S(1)}, bf16[16,8448]{1,0:T(8,128)(2,1)S(1)}, u32[]{:S(2)}, u32[]{:S(2)}) collective-permute-start(bf16[16,8448]{1,0:T(8,128)(2,1)S(1)} %collective-permute-done.refs_3_), channel_id=1, source_target_pairs={{0,56},{8,0},{16,8},{24,16},{32,24},{40,32},{48,40},{56,48},{64,12... | collective-permute-start | bytes 811016 | tf_op jit(solution)/shard_map/ppermute | solution.py:146
  14.0 1.5 %collective-permute-start.29 = (bf16[16,8448]{1,0:T(8,128)(2,1)S(1)}, bf16[16,8448]{1,0:T(8,128)(2,1)S(1)}, u32[]{:S(2)}, u32[]{:S(2)}) collective-permute-start(bf16[16,8448]{1,0:T(8,128)(2,1)S(1)} %collective-permute-done.5.refs_4_), channel_id=1, source_target_pairs={{0,192},{8,200},{16,208},{24,216},{32,224},{40,232},{48,240},{56,2... | collective-permute-start | bytes 811016 | tf_op jit(solution)/shard_map/ppermute | solution.py:146
  16.4 3.0 %collective-permute-done.6.refs_8_ = bf16[16,8448]{1,0:T(8,128)(2,1)S(1)} collective-permute-done((bf16[16,8448]{1,0:T(8,128)(2,1)S(1)}, bf16[16,8448]{1,0:T(8,128)(2,1)S(1)}, u32[]{:S(2)}, u32[]{:S(2)}) %collective-permute-start.6) | collective-permute-done | bytes 270368 | tf_op jit(solution)/shard_map/ppermute | solution.py:146
  19.4 3.0 %collective-permute-start.28 = (bf16[16,8448]{1,0:T(8,128)(2,1)S(1)}, bf16[16,8448]{1,0:T(8,128)(2,1)S(1)}, u32[]{:S(2)}, u32[]{:S(2)}) collective-permute-start(bf16[16,8448]{1,0:T(8,128)(2,1)S(1)} %collective-permute-done.25.refs_5_), channel_id=1, source_target_pairs={{0,56},{8,0},{16,8},{24,16},{32,24},{40,32},{48,40},{56,48},{64,12... | collective-permute-start | bytes 811016 | tf_op jit(solution)/shard_map/ppermute | solution.py:146
  22.9 1.9 %collective-permute-start.10 = (bf16[16,8448]{1,0:T(8,128)(2,1)S(1)}, bf16[16,8448]{1,0:T(8,128)(2,1)S(1)}, u32[]{:S(2)}, u32[]{:S(2)}) collective-permute-start(bf16[16,8448]{1,0:T(8,128)(2,1)S(1)} %collective-permute-done.6.refs_8_), channel_id=1, source_target_pairs={{0,8},{8,16},{16,24},{24,32},{32,40},{40,48},{48,56},{56,0},{64,72... | collective-permute-start | bytes 811016 | tf_op jit(solution)/shard_map/ppermute | solution.py:146
  24.8 3.0 %collective-permute-start.13 = (bf16[16,8448]{1,0:T(8,128)(2,1)S(1)}, bf16[16,8448]{1,0:T(8,128)(2,1)S(1)}, u32[]{:S(2)}, u32[]{:S(2)}) collective-permute-start(bf16[16,8448]{1,0:T(8,128)(2,1)S(1)} %collective-permute-done.1.refs_7_), channel_id=1, source_target_pairs={{0,56},{8,0},{16,8},{24,16},{32,24},{40,32},{48,40},{56,48},{64,12... | collective-permute-start | bytes 811016 | tf_op jit(solution)/shard_map/ppermute | solution.py:146
  29.9 2.4 %collective-permute-start.30 = (bf16[16,8448]{1,0:T(8,128)(2,1)S(1)}, bf16[16,8448]{1,0:T(8,128)(2,1)S(1)}, u32[]{:S(2)}, u32[]{:S(2)}) collective-permute-start(bf16[16,8448]{1,0:T(8,128)(2,1)S(1)} %collective-permute-done.15.refs_9_), channel_id=1, source_target_pairs={{0,8},{8,16},{16,24},{24,32},{32,40},{40,48},{48,56},{56,0},{64,72... | collective-permute-start | bytes 811016 | tf_op jit(solution)/shard_map/ppermute | solution.py:146
  32.3 1.3 %collective-permute-start.2 = (bf16[16,8448]{1,0:T(8,128)(2,1)S(1)}, bf16[16,8448]{1,0:T(8,128)(2,1)S(1)}, u32[]{:S(2)}, u32[]{:S(2)}) collective-permute-start(bf16[16,8448]{1,0:T(8,128)(2,1)S(1)} %collective-permute-done.1.refs_7_), channel_id=1, source_target_pairs={{0,192},{8,200},{16,208},{24,216},{32,224},{40,232},{48,240},{56,2... | collective-permute-start | bytes 811016 | tf_op jit(solution)/shard_map/ppermute | solution.py:146
  33.9 3.6 %collective-permute-done.3.refs_13_ = bf16[16,8448]{1,0:T(8,128)(2,1)S(1)} collective-permute-done((bf16[16,8448]{1,0:T(8,128)(2,1)S(1)}, bf16[16,8448]{1,0:T(8,128)(2,1)S(1)}, u32[]{:S(2)}, u32[]{:S(2)}) %collective-permute-start.3) | collective-permute-done | bytes 270368 | tf_op jit(solution)/shard_map/ppermute | solution.py:146
  37.5 2.4 %collective-permute-start.4 = (bf16[16,8448]{1,0:T(8,128)(2,1)S(1)}, bf16[16,8448]{1,0:T(8,128)(2,1)S(1)}, u32[]{:S(2)}, u32[]{:S(2)}) collective-permute-start(bf16[16,8448]{1,0:T(8,128)(2,1)S(1)} %collective-permute-done.3.refs_13_), channel_id=1, source_target_pairs={{0,56},{8,0},{16,8},{24,16},{32,24},{40,32},{48,40},{56,48},{64,12... | collective-permute-start | bytes 811016 | tf_op jit(solution)/shard_map/ppermute | solution.py:146
  40.6 1.6 %collective-permute-start.8 = (bf16[16,8448]{1,0:T(8,128)(2,1)S(1)}, bf16[16,8448]{1,0:T(8,128)(2,1)}, u32[]{:S(2)}, u32[]{:S(2)}) collective-permute-start(bf16[16,8448]{1,0:T(8,128)(2,1)S(1)} %collective-permute-done.3.refs_13_), channel_id=1, source_target_pairs={{0,64},{8,72},{16,80},{24,88},{32,96},{40,104},{48,112},{56,120},{... | collective-permute-start | bytes 811016 | tf_op jit(solution)/shard_map/ppermute | solution.py:146
  44.7 2.8 %collective-permute-start.11 = (bf16[16,8448]{1,0:T(8,128)(2,1)S(1)}, bf16[16,8448]{1,0:T(8,128)(2,1)S(1)}, u32[]{:S(2)}, u32[]{:S(2)}) collective-permute-start(bf16[16,8448]{1,0:T(8,128)(2,1)S(1)} %collective-permute-done.10.refs_15_), channel_id=1, source_target_pairs={{0,64},{8,72},{16,80},{24,88},{32,96},{40,104},{48,112},{56,120},{... | collective-permute-start | bytes 811016 | tf_op jit(solution)/shard_map/ppermute | solution.py:146
  48.2 2.1 %collective-permute-start.14 = (bf16[16,8448]{1,0:T(8,128)(2,1)S(1)}, bf16[16,8448]{1,0:T(8,128)(2,1)S(1)}, u32[]{:S(2)}, u32[]{:S(2)}) collective-permute-start(bf16[16,8448]{1,0:T(8,128)(2,1)S(1)} %collective-permute-done.13.refs_14_), channel_id=1, source_target_pairs={{0,56},{8,0},{16,8},{24,16},{32,24},{40,32},{48,40},{56,48},{64,12... | collective-permute-start | bytes 811016 | tf_op jit(solution)/shard_map/ppermute | solution.py:146
  52.8 2.2 %collective-permute-start.18 = (bf16[16,8448]{1,0:T(8,128)(2,1)S(1)}, bf16[16,8448]{1,0:T(8,128)(2,1)}, u32[]{:S(2)}, u32[]{:S(2)}) collective-permute-start(bf16[16,8448]{1,0:T(8,128)(2,1)S(1)} %collective-permute-done.4.refs_3_), channel_id=1, source_target_pairs={{0,56},{8,0},{16,8},{24,16},{32,24},{40,32},{48,40},{56,48},{64,12... | collective-permute-start | bytes 811016 | tf_op jit(solution)/shard_map/ppermute | solution.py:146
  56.4 2.2 %collective-permute-start.19 = (bf16[16,8448]{1,0:T(8,128)(2,1)}, bf16[16,8448]{1,0:T(8,128)(2,1)}, u32[]{:S(2)}, u32[]{:S(2)}) collective-permute-start(bf16[16,8448]{1,0:T(8,128)(2,1)} %collective-permute-done.8.refs_5_), channel_id=1, source_target_pairs={{0,56},{8,0},{16,8},{24,16},{32,24},{40,32},{48,40},{56,48},{64,12... | collective-permute-start | bytes 811016 | tf_op jit(solution)/shard_map/ppermute | solution.py:146
  60.5 3.5 %collective-permute-start.22 = (bf16[16,8448]{1,0:T(8,128)(2,1)}, bf16[16,8448]{1,0:T(8,128)(2,1)}, u32[]{:S(2)}, u32[]{:S(2)}) collective-permute-start(bf16[16,8448]{1,0:T(8,128)(2,1)} %collective-permute-done.12.refs_8_), channel_id=1, source_target_pairs={{0,8},{8,16},{16,24},{24,32},{32,40},{40,48},{48,56},{56,0},{64,72... | collective-permute-start | bytes 811016 | tf_op jit(solution)/shard_map/ppermute | solution.py:146
  64.8 3.2 %collective-permute-start.24 = (bf16[16,8448]{1,0:T(8,128)(2,1)}, bf16[16,8448]{1,0:T(8,128)(2,1)}, u32[]{:S(2)}, u32[]{:S(2)}) collective-permute-start(bf16[16,8448]{1,0:T(8,128)(2,1)} %collective-permute-done.18.refs_11_), channel_id=1, source_target_pairs={{0,64},{8,72},{16,80},{24,88},{32,96},{40,104},{48,112},{56,120},{... | collective-permute-start | bytes 811016 | tf_op jit(solution)/shard_map/ppermute | solution.py:146
  68.0 2.2 %copy-done = bf16[1,512,4096]{2,1,0:T(8,128)(2,1)S(1)} copy-done((bf16[1,512,4096]{2,1,0:T(8,128)(2,1)S(1)}, bf16[1,512,4096]{2,1,0:T(8,128)(2,1)}, u32[]{:S(2)}) %copy-start) | copy-done | bytes 4194328
  70.2 2.2 %copy-done.2 = bf16[1,512,4096]{2,1,0:T(8,128)(2,1)S(1)} copy-done((bf16[1,512,4096]{2,1,0:T(8,128)(2,1)S(1)}, bf16[1,512,4096]{2,1,0:T(8,128)(2,1)}, u32[]{:S(2)}) %copy-start.2) | copy-done | bytes 4194328
  72.5 2.2 %copy-done.1 = bf16[1,512,4096]{2,1,0:T(8,128)(2,1)S(1)} copy-done((bf16[1,512,4096]{2,1,0:T(8,128)(2,1)S(1)}, bf16[1,512,4096]{2,1,0:T(8,128)(2,1)}, u32[]{:S(2)}) %copy-start.1) | copy-done | bytes 4194328
  74.7 2.2 %copy-done.3 = bf16[1,512,4096]{2,1,0:T(8,128)(2,1)S(1)} copy-done((bf16[1,512,4096]{2,1,0:T(8,128)(2,1)S(1)}, bf16[1,512,4096]{2,1,0:T(8,128)(2,1)}, u32[]{:S(2)}) %copy-start.3) | copy-done | bytes 4194328
  80.7 2.6 %shard_map.60.refs_18_ = f32[512,256]{1,0:T(8,128)S(1)} custom-call(bf16[16,128]{1,0:T(8,128)(2,1)S(1)} %shard_map.55.refs_0_.tag, bf16[512,4096]{1,0:T(8,128)(2,1)S(1)} %bitcast.25, bf16[512,4096]{1,0:T(8,128)(2,1)S(1)} %bitcast.32, bf16[16,8448]{1,0:T(8,128)(2,1)S(1)} %pad_maximum_fusion.refs_2_, bf16[16,8448]{1,0:T(8,128)(2,1)S(1)} %collective-permute-done.refs_3_, ...), custom_call_target="tpu_custom_call" | custom-call | flops 1 | bytes 1 | tf_op jit(solution)/shard_map/pallas_call | solution.py:123
  83.4 4.1 %shard_map.61 = f32[512,256]{1,0:T(8,128)S(1)} custom-call(bf16[16,128]{1,0:T(8,128)(2,1)S(1)} %shard_map.59.tag, bf16[512,4096]{1,0:T(8,128)(2,1)S(1)} %bitcast.26, bf16[512,4096]{1,0:T(8,128)(2,1)S(1)} %bitcast.33, bf16[16,8448]{1,0:T(8,128)(2,1)S(1)} %copy-done.9, bf16[16,8448]{1,0:T(8,128)(2,1)S(1)} %copy-done.17, bf16[16,8448]{1,0:T(8,128)(2,1)S(1)} %copy-done.13, ...), custom_call_target="tpu_custom_call" | custom-call | flops 1 | bytes 1 | tf_op jit(solution)/shard_map/pallas_call | solution.py:123
  87.7 1.5 %collective-permute-done.31 = f32[2,128,256]{2,1,0:T(8,128)S(1)} collective-permute-done((f32[2,128,256]{2,1,0:T(8,128)S(1)}, f32[2,128,256]{2,1,0:T(8,128)S(1)}, u32[]{:S(2)}, u32[]{:S(2)}) %collective-permute-start.31) | collective-permute-done | bytes 262176 | tf_op jit(solution)/shard_map/ppermute | solution.py:159
  89.2 1.7 %collective-permute-start.32 = (bf16[128,256]{1,0:T(8,128)(2,1)S(1)}, bf16[128,256]{1,0:T(8,128)(2,1)S(1)}, u32[]{:S(2)}, u32[]{:S(2)}) collective-permute-start(bf16[128,256]{1,0:T(8,128)(2,1)S(1)} %get-tuple-element.5), channel_id=1, source_target_pairs={{0,4},{1,5},{2,6},{3,7},{4,0},{5,1},{6,2},{7,3},{8,12},{9,13},{10,... | collective-permute-start | bytes 196616 | tf_op jit(solution)/shard_map/ppermute | solution.py:169
  90.9 2.2 %collective-permute-start.33 = (bf16[128,256]{1,0:T(8,128)(2,1)S(1)}, bf16[128,256]{1,0:T(8,128)(2,1)S(1)}, u32[]{:S(2)}, u32[]{:S(2)}) collective-permute-start(bf16[128,256]{1,0:T(8,128)(2,1)S(1)} %get-tuple-element.6), channel_id=1, source_target_pairs={{0,6},{1,7},{2,4},{3,5},{4,2},{5,3},{6,0},{7,1},{8,14},{9,15},{10,... | collective-permute-start | bytes 196616 | tf_op jit(solution)/shard_map/ppermute | solution.py:169
  93.8 2.6 %collective-permute-done.33 = bf16[128,256]{1,0:T(8,128)(2,1)S(1)} collective-permute-done((bf16[128,256]{1,0:T(8,128)(2,1)S(1)}, bf16[128,256]{1,0:T(8,128)(2,1)S(1)}, u32[]{:S(2)}, u32[]{:S(2)}) %collective-permute-start.33) | collective-permute-done | bytes 65568 | tf_op jit(solution)/shard_map/ppermute | solution.py:169
  96.4 2.5 %collective-permute-done.34 = bf16[128,256]{1,0:T(8,128)(2,1)S(1)} collective-permute-done((bf16[128,256]{1,0:T(8,128)(2,1)S(1)}, bf16[128,256]{1,0:T(8,128)(2,1)S(1)}, u32[]{:S(2)}, u32[]{:S(2)}) %collective-permute-start.34) | collective-permute-done | bytes 65568 | tf_op jit(solution)/shard_map/ppermute | solution.py:169
  (102 shorter events, 21.9 us)
Async XLA Ops:
  1.0 8.3 %collective-permute-start.5 = (bf16[16,8448]{1,0:T(8,128)(2,1)S(1)}, bf16[16,8448]{1,0:T(8,128)(2,1)S(1)}, u32[]{:S(2)}, u32[]{:S(2)}) collective-permute-start(bf16[16,8448]{1,0:T(8,128)(2,1)S(1)} %pad_maximum_fusion.refs_2_), channel_id=1, source_target_pairs={{0,8},{8,16},{16,24},{24,32},{32,40},{40,48},{48,56},{56,0},{64,72... | collective-permute-start | bytes 811016 | tf_op jit(solution)/shard_map/ppermute | solution.py:146
  3.0 8.2 %collective-permute-start = (bf16[16,8448]{1,0:T(8,128)(2,1)S(1)}, bf16[16,8448]{1,0:T(8,128)(2,1)S(1)}, u32[]{:S(2)}, u32[]{:S(2)}) collective-permute-start(bf16[16,8448]{1,0:T(8,128)(2,1)S(1)} %pad_maximum_fusion.refs_2_), channel_id=1, source_target_pairs={{0,56},{8,0},{16,8},{24,16},{32,24},{40,32},{48,40},{56,48},{64,12... | collective-permute-start | bytes 811016 | tf_op jit(solution)/shard_map/ppermute | solution.py:146
  3.1 10.9 %collective-permute-start.25 = (bf16[16,8448]{1,0:T(8,128)(2,1)S(1)}, bf16[16,8448]{1,0:T(8,128)(2,1)S(1)}, u32[]{:S(2)}, u32[]{:S(2)}) collective-permute-start(bf16[16,8448]{1,0:T(8,128)(2,1)S(1)} %pad_maximum_fusion.refs_2_), channel_id=1, source_target_pairs={{0,192},{8,200},{16,208},{24,216},{32,224},{40,232},{48,240},{56,2... | collective-permute-start | bytes 811016 | tf_op jit(solution)/shard_map/ppermute | solution.py:146
  3.9 11.6 %collective-permute-start.26 = (bf16[16,8448]{1,0:T(8,128)(2,1)S(1)}, bf16[16,8448]{1,0:T(8,128)(2,1)S(1)}, u32[]{:S(2)}, u32[]{:S(2)}) collective-permute-start(bf16[16,8448]{1,0:T(8,128)(2,1)S(1)} %pad_maximum_fusion.refs_2_), channel_id=1, source_target_pairs={{0,64},{8,72},{16,80},{24,88},{32,96},{40,104},{48,112},{56,120},{... | collective-permute-start | bytes 811016 | tf_op jit(solution)/shard_map/ppermute | solution.py:146
  9.3 10.1 %collective-permute-start.6 = (bf16[16,8448]{1,0:T(8,128)(2,1)S(1)}, bf16[16,8448]{1,0:T(8,128)(2,1)S(1)}, u32[]{:S(2)}, u32[]{:S(2)}) collective-permute-start(bf16[16,8448]{1,0:T(8,128)(2,1)S(1)} %collective-permute-done.5.refs_4_), channel_id=1, source_target_pairs={{0,8},{8,16},{16,24},{24,32},{32,40},{40,48},{48,56},{56,0},{64,72... | collective-permute-start | bytes 811016 | tf_op jit(solution)/shard_map/ppermute | solution.py:146
  11.2 11.2 %collective-permute-start.1 = (bf16[16,8448]{1,0:T(8,128)(2,1)S(1)}, bf16[16,8448]{1,0:T(8,128)(2,1)S(1)}, u32[]{:S(2)}, u32[]{:S(2)}) collective-permute-start(bf16[16,8448]{1,0:T(8,128)(2,1)S(1)} %collective-permute-done.refs_3_), channel_id=1, source_target_pairs={{0,56},{8,0},{16,8},{24,16},{32,24},{40,32},{48,40},{56,48},{64,12... | collective-permute-start | bytes 811016 | tf_op jit(solution)/shard_map/ppermute | solution.py:146
  13.5 9.3 %collective-permute-start.15 = (bf16[16,8448]{1,0:T(8,128)(2,1)S(1)}, bf16[16,8448]{1,0:T(8,128)(2,1)S(1)}, u32[]{:S(2)}, u32[]{:S(2)}) collective-permute-start(bf16[16,8448]{1,0:T(8,128)(2,1)S(1)} %collective-permute-done.5.refs_4_), channel_id=1, source_target_pairs={{0,64},{8,72},{16,80},{24,88},{32,96},{40,104},{48,112},{56,120},{... | collective-permute-start | bytes 811016 | tf_op jit(solution)/shard_map/ppermute | solution.py:146
  14.0 10.8 %collective-permute-start.29 = (bf16[16,8448]{1,0:T(8,128)(2,1)S(1)}, bf16[16,8448]{1,0:T(8,128)(2,1)S(1)}, u32[]{:S(2)}, u32[]{:S(2)}) collective-permute-start(bf16[16,8448]{1,0:T(8,128)(2,1)S(1)} %collective-permute-done.5.refs_4_), channel_id=1, source_target_pairs={{0,192},{8,200},{16,208},{24,216},{32,224},{40,232},{48,240},{56,2... | collective-permute-start | bytes 811016 | tf_op jit(solution)/shard_map/ppermute | solution.py:146
  15.6 12.5 %collective-permute-start.27 = (bf16[16,8448]{1,0:T(8,128)(2,1)S(1)}, bf16[16,8448]{1,0:T(8,128)(2,1)S(1)}, u32[]{:S(2)}, u32[]{:S(2)}) collective-permute-start(bf16[16,8448]{1,0:T(8,128)(2,1)S(1)} %collective-permute-done.25.refs_5_), channel_id=1, source_target_pairs={{0,192},{8,200},{16,208},{24,216},{32,224},{40,232},{48,240},{56,2... | collective-permute-start | bytes 811016 | tf_op jit(solution)/shard_map/ppermute | solution.py:146
  19.4 9.8 %collective-permute-start.28 = (bf16[16,8448]{1,0:T(8,128)(2,1)S(1)}, bf16[16,8448]{1,0:T(8,128)(2,1)S(1)}, u32[]{:S(2)}, u32[]{:S(2)}) collective-permute-start(bf16[16,8448]{1,0:T(8,128)(2,1)S(1)} %collective-permute-done.25.refs_5_), channel_id=1, source_target_pairs={{0,56},{8,0},{16,8},{24,16},{32,24},{40,32},{48,40},{56,48},{64,12... | collective-permute-start | bytes 811016 | tf_op jit(solution)/shard_map/ppermute | solution.py:146
  22.4 7.5 %collective-permute-start.9 = (bf16[16,8448]{1,0:T(8,128)(2,1)S(1)}, bf16[16,8448]{1,0:T(8,128)(2,1)S(1)}, u32[]{:S(2)}, u32[]{:S(2)}) collective-permute-start(bf16[16,8448]{1,0:T(8,128)(2,1)S(1)} %collective-permute-done.refs_3_), channel_id=1, source_target_pairs={{0,64},{8,72},{16,80},{24,88},{32,96},{40,104},{48,112},{56,120},{... | collective-permute-start | bytes 811016 | tf_op jit(solution)/shard_map/ppermute | solution.py:146
  22.9 9.4 %collective-permute-start.10 = (bf16[16,8448]{1,0:T(8,128)(2,1)S(1)}, bf16[16,8448]{1,0:T(8,128)(2,1)S(1)}, u32[]{:S(2)}, u32[]{:S(2)}) collective-permute-start(bf16[16,8448]{1,0:T(8,128)(2,1)S(1)} %collective-permute-done.6.refs_8_), channel_id=1, source_target_pairs={{0,8},{8,16},{16,24},{24,32},{32,40},{40,48},{48,56},{56,0},{64,72... | collective-permute-start | bytes 811016 | tf_op jit(solution)/shard_map/ppermute | solution.py:146
  24.8 8.8 %collective-permute-start.13 = (bf16[16,8448]{1,0:T(8,128)(2,1)S(1)}, bf16[16,8448]{1,0:T(8,128)(2,1)S(1)}, u32[]{:S(2)}, u32[]{:S(2)}) collective-permute-start(bf16[16,8448]{1,0:T(8,128)(2,1)S(1)} %collective-permute-done.1.refs_7_), channel_id=1, source_target_pairs={{0,56},{8,0},{16,8},{24,16},{32,24},{40,32},{48,40},{56,48},{64,12... | collective-permute-start | bytes 811016 | tf_op jit(solution)/shard_map/ppermute | solution.py:146
  28.1 9.4 %collective-permute-start.3 = (bf16[16,8448]{1,0:T(8,128)(2,1)S(1)}, bf16[16,8448]{1,0:T(8,128)(2,1)S(1)}, u32[]{:S(2)}, u32[]{:S(2)}) collective-permute-start(bf16[16,8448]{1,0:T(8,128)(2,1)S(1)} %collective-permute-done.1.refs_7_), channel_id=1, source_target_pairs={{0,64},{8,72},{16,80},{24,88},{32,96},{40,104},{48,112},{56,120},{... | collective-permute-start | bytes 811016 | tf_op jit(solution)/shard_map/ppermute | solution.py:146
  29.3 11.3 %collective-permute-start.16 = (bf16[16,8448]{1,0:T(8,128)(2,1)S(1)}, bf16[16,8448]{1,0:T(8,128)(2,1)S(1)}, u32[]{:S(2)}, u32[]{:S(2)}) collective-permute-start(bf16[16,8448]{1,0:T(8,128)(2,1)S(1)} %collective-permute-done.15.refs_9_), channel_id=1, source_target_pairs={{0,64},{8,72},{16,80},{24,88},{32,96},{40,104},{48,112},{56,120},{... | collective-permute-start | bytes 811016 | tf_op jit(solution)/shard_map/ppermute | solution.py:146
  29.9 13.0 %collective-permute-start.30 = (bf16[16,8448]{1,0:T(8,128)(2,1)S(1)}, bf16[16,8448]{1,0:T(8,128)(2,1)S(1)}, u32[]{:S(2)}, u32[]{:S(2)}) collective-permute-start(bf16[16,8448]{1,0:T(8,128)(2,1)S(1)} %collective-permute-done.15.refs_9_), channel_id=1, source_target_pairs={{0,8},{8,16},{16,24},{24,32},{32,40},{40,48},{48,56},{56,0},{64,72... | collective-permute-start | bytes 811016 | tf_op jit(solution)/shard_map/ppermute | solution.py:146
  32.3 11.7 %collective-permute-start.2 = (bf16[16,8448]{1,0:T(8,128)(2,1)S(1)}, bf16[16,8448]{1,0:T(8,128)(2,1)S(1)}, u32[]{:S(2)}, u32[]{:S(2)}) collective-permute-start(bf16[16,8448]{1,0:T(8,128)(2,1)S(1)} %collective-permute-done.1.refs_7_), channel_id=1, source_target_pairs={{0,192},{8,200},{16,208},{24,216},{32,224},{40,232},{48,240},{56,2... | collective-permute-start | bytes 811016 | tf_op jit(solution)/shard_map/ppermute | solution.py:146
  33.6 13.9 %collective-permute-start.7 = (bf16[16,8448]{1,0:T(8,128)(2,1)S(1)}, bf16[16,8448]{1,0:T(8,128)(2,1)S(1)}, u32[]{:S(2)}, u32[]{:S(2)}) collective-permute-start(bf16[16,8448]{1,0:T(8,128)(2,1)S(1)} %collective-permute-done.6.refs_8_), channel_id=1, source_target_pairs={{0,192},{8,200},{16,208},{24,216},{32,224},{40,232},{48,240},{56,2... | collective-permute-start | bytes 811016 | tf_op jit(solution)/shard_map/ppermute | solution.py:146
  37.5 12.9 %collective-permute-start.4 = (bf16[16,8448]{1,0:T(8,128)(2,1)S(1)}, bf16[16,8448]{1,0:T(8,128)(2,1)S(1)}, u32[]{:S(2)}, u32[]{:S(2)}) collective-permute-start(bf16[16,8448]{1,0:T(8,128)(2,1)S(1)} %collective-permute-done.3.refs_13_), channel_id=1, source_target_pairs={{0,56},{8,0},{16,8},{24,16},{32,24},{40,32},{48,40},{56,48},{64,12... | collective-permute-start | bytes 811016 | tf_op jit(solution)/shard_map/ppermute | solution.py:146
  40.6 10.6 %collective-permute-start.8 = (bf16[16,8448]{1,0:T(8,128)(2,1)S(1)}, bf16[16,8448]{1,0:T(8,128)(2,1)}, u32[]{:S(2)}, u32[]{:S(2)}) collective-permute-start(bf16[16,8448]{1,0:T(8,128)(2,1)S(1)} %collective-permute-done.3.refs_13_), channel_id=1, source_target_pairs={{0,64},{8,72},{16,80},{24,88},{32,96},{40,104},{48,112},{56,120},{... | collective-permute-start | bytes 811016 | tf_op jit(solution)/shard_map/ppermute | solution.py:146
  43.6 9.3 %collective-permute-start.12 = (bf16[16,8448]{1,0:T(8,128)(2,1)S(1)}, bf16[16,8448]{1,0:T(8,128)(2,1)}, u32[]{:S(2)}, u32[]{:S(2)}) collective-permute-start(bf16[16,8448]{1,0:T(8,128)(2,1)S(1)} %collective-permute-done.10.refs_15_), channel_id=1, source_target_pairs={{0,192},{8,200},{16,208},{24,216},{32,224},{40,232},{48,240},{56,2... | collective-permute-start | bytes 811016 | tf_op jit(solution)/shard_map/ppermute | solution.py:146
  44.7 11.0 %collective-permute-start.11 = (bf16[16,8448]{1,0:T(8,128)(2,1)S(1)}, bf16[16,8448]{1,0:T(8,128)(2,1)S(1)}, u32[]{:S(2)}, u32[]{:S(2)}) collective-permute-start(bf16[16,8448]{1,0:T(8,128)(2,1)S(1)} %collective-permute-done.10.refs_15_), channel_id=1, source_target_pairs={{0,64},{8,72},{16,80},{24,88},{32,96},{40,104},{48,112},{56,120},{... | collective-permute-start | bytes 811016 | tf_op jit(solution)/shard_map/ppermute | solution.py:146
  48.2 10.4 %collective-permute-start.14 = (bf16[16,8448]{1,0:T(8,128)(2,1)S(1)}, bf16[16,8448]{1,0:T(8,128)(2,1)S(1)}, u32[]{:S(2)}, u32[]{:S(2)}) collective-permute-start(bf16[16,8448]{1,0:T(8,128)(2,1)S(1)} %collective-permute-done.13.refs_14_), channel_id=1, source_target_pairs={{0,56},{8,0},{16,8},{24,16},{32,24},{40,32},{48,40},{56,48},{64,12... | collective-permute-start | bytes 811016 | tf_op jit(solution)/shard_map/ppermute | solution.py:146
  50.4 9.5 %collective-permute-start.21 = (bf16[16,8448]{1,0:T(8,128)(2,1)S(1)}, bf16[16,8448]{1,0:T(8,128)(2,1)S(1)}, u32[]{:S(2)}, u32[]{:S(2)}) collective-permute-start(bf16[16,8448]{1,0:T(8,128)(2,1)S(1)} %collective-permute-done.13.refs_14_), channel_id=1, source_target_pairs={{0,192},{8,200},{16,208},{24,216},{32,224},{40,232},{48,240},{56,2... | collective-permute-start | bytes 811016 | tf_op jit(solution)/shard_map/ppermute | solution.py:146
  51.1 12.9 %collective-permute-start.17 = (bf16[16,8448]{1,0:T(8,128)(2,1)S(1)}, bf16[16,8448]{1,0:T(8,128)(2,1)S(1)}, u32[]{:S(2)}, u32[]{:S(2)}) collective-permute-start(bf16[16,8448]{1,0:T(8,128)(2,1)S(1)} %collective-permute-done.16.refs_17_), channel_id=1, source_target_pairs={{0,8},{8,16},{16,24},{24,32},{32,40},{40,48},{48,56},{56,0},{64,72... | collective-permute-start | bytes 811016 | tf_op jit(solution)/shard_map/ppermute | solution.py:146
  52.8 11.9 %collective-permute-start.18 = (bf16[16,8448]{1,0:T(8,128)(2,1)S(1)}, bf16[16,8448]{1,0:T(8,128)(2,1)}, u32[]{:S(2)}, u32[]{:S(2)}) collective-permute-start(bf16[16,8448]{1,0:T(8,128)(2,1)S(1)} %collective-permute-done.4.refs_3_), channel_id=1, source_target_pairs={{0,56},{8,0},{16,8},{24,16},{32,24},{40,32},{48,40},{56,48},{64,12... | collective-permute-start | bytes 811016 | tf_op jit(solution)/shard_map/ppermute | solution.py:146
  56.4 26.9 %collective-permute-start.19 = (bf16[16,8448]{1,0:T(8,128)(2,1)}, bf16[16,8448]{1,0:T(8,128)(2,1)}, u32[]{:S(2)}, u32[]{:S(2)}) collective-permute-start(bf16[16,8448]{1,0:T(8,128)(2,1)} %collective-permute-done.8.refs_5_), channel_id=1, source_target_pairs={{0,56},{8,0},{16,8},{24,16},{32,24},{40,32},{48,40},{56,48},{64,12... | collective-permute-start | bytes 811016 | tf_op jit(solution)/shard_map/ppermute | solution.py:146
  59.4 23.9 %collective-permute-start.20 = (bf16[16,8448]{1,0:T(8,128)(2,1)}, bf16[16,8448]{1,0:T(8,128)(2,1)}, u32[]{:S(2)}, u32[]{:S(2)}) collective-permute-start(bf16[16,8448]{1,0:T(8,128)(2,1)} %collective-permute-done.8.refs_5_), channel_id=1, source_target_pairs={{0,8},{8,16},{16,24},{24,32},{32,40},{40,48},{48,56},{56,0},{64,72... | collective-permute-start | bytes 811016 | tf_op jit(solution)/shard_map/ppermute | solution.py:146
  60.5 22.7 %collective-permute-start.22 = (bf16[16,8448]{1,0:T(8,128)(2,1)}, bf16[16,8448]{1,0:T(8,128)(2,1)}, u32[]{:S(2)}, u32[]{:S(2)}) collective-permute-start(bf16[16,8448]{1,0:T(8,128)(2,1)} %collective-permute-done.12.refs_8_), channel_id=1, source_target_pairs={{0,8},{8,16},{16,24},{24,32},{32,40},{40,48},{48,56},{56,0},{64,72... | collective-permute-start | bytes 811016 | tf_op jit(solution)/shard_map/ppermute | solution.py:146
  64.8 18.5 %collective-permute-start.23 = (bf16[16,8448]{1,0:T(8,128)(2,1)}, bf16[16,8448]{1,0:T(8,128)(2,1)}, u32[]{:S(2)}, u32[]{:S(2)}) collective-permute-start(bf16[16,8448]{1,0:T(8,128)(2,1)} %collective-permute-done.12.refs_8_), channel_id=1, source_target_pairs={{0,192},{8,200},{16,208},{24,216},{32,224},{40,232},{48,240},{56,2... | collective-permute-start | bytes 811016 | tf_op jit(solution)/shard_map/ppermute | solution.py:146
  64.8 18.5 %collective-permute-start.24 = (bf16[16,8448]{1,0:T(8,128)(2,1)}, bf16[16,8448]{1,0:T(8,128)(2,1)}, u32[]{:S(2)}, u32[]{:S(2)}) collective-permute-start(bf16[16,8448]{1,0:T(8,128)(2,1)} %collective-permute-done.18.refs_11_), channel_id=1, source_target_pairs={{0,64},{8,72},{16,80},{24,88},{32,96},{40,104},{48,112},{56,120},{... | collective-permute-start | bytes 811016 | tf_op jit(solution)/shard_map/ppermute | solution.py:146
  93.1 5.8 %collective-permute-start.34 = (bf16[128,256]{1,0:T(8,128)(2,1)S(1)}, bf16[128,256]{1,0:T(8,128)(2,1)S(1)}, u32[]{:S(2)}, u32[]{:S(2)}) collective-permute-start(bf16[128,256]{1,0:T(8,128)(2,1)S(1)} %get-tuple-element.6), channel_id=1, source_target_pairs={{0,2},{1,3},{2,0},{3,1},{4,6},{5,7},{6,4},{7,5},{8,10},{9,11},{10,... | collective-permute-start | bytes 196616 | tf_op jit(solution)/shard_map/ppermute | solution.py:169
  (29 other events, 50.8 us)
